TPU v7x, 512 devices: a whole 4x4x16 slice. The times are simulated.
512 devices in a mesh: blk: 16 (over x, y_hi, core), vox: 32 (over z, y_lo).
Axes of the slice: x: 4, y: 4 (y_hi: 2, y_lo: 2; y = y_hi * 2 + y_lo), z: 16, core: 2. Of those that a mesh axis runs over, the one named last changes fastest.
Arguments:
- src_fields: bfloat16 [1024, 131072], P('blk', 'vox'), may hold values from -6 to 6
- det_fields: bfloat16 [1024, 131072], P('blk', 'vox'), may hold values from -6 to 6
- probes: bfloat16 [2, 131072], P(None, 'vox'), may hold values from -6 to 6
Outputs:
- curvature: float32 [2, 131072], P(None, 'vox')
All inputs are finite; a program needn't handle non-finite values.
Results may differ from a plain program's by a relative error of at most 0.0016.
Values may be sent and summed in bfloat16 or wider, within the bound.
A program may use at most 64 MiB of HBM per device.

v0:
```python
import jax
import jax.numpy as jnp
from jax import lax
from jax.sharding import PartitionSpec as P


def rows_for(lines, count):
    spare = -lines.shape[0] % count
    if not spare:
        return lines
    return jnp.concatenate([lines, jnp.zeros((spare, *lines.shape[1:]), lines.dtype)])


def from_everyone(value, axis):
    copies = jnp.broadcast_to(value, (lax.axis_size(axis), *value.shape))
    return lax.all_to_all(copies, axis, split_axis=0, concat_axis=0, tiled=True)


def laid_out(tiles, dim):
    lengths = list(tiles.shape[1:])
    lengths[dim] *= tiles.shape[0]
    return jnp.moveaxis(tiles, 0, dim).reshape(lengths)


def gathered_copies(value, axis, dim):
    tiles = from_everyone(value, axis)
    return laid_out(tiles, dim)


def cut_along(value, dim, count):
    before, after = (value.shape[:dim], value.shape[dim + 1 :])
    return jnp.moveaxis(value.reshape(*before, count, -1, *after), dim, 0)


def summed_on_arrival(value, axis, dim):
    count = lax.axis_size(axis)
    tiles = lax.all_to_all(cut_along(value, dim, count), axis, 0, 0, tiled=True)
    return jnp.sum(tiles, axis=0)


def total_of(value, axes):
    lines = value.reshape(-1, value.shape[-1])
    padded = rows_for(lines, lax.axis_size(axes))
    whole = gathered_copies(summed_on_arrival(padded, axes, 0), axes, 0)
    return lax.slice_in_dim(whole, 0, len(lines)).reshape(value.shape)


def of_everyone(value, axis):
    everything = from_everyone(value, axis)
    return jnp.sum(everything, axis=0)


def shards(src_fields, det_fields, probes):
    src_count, vox_count = src_fields.shape
    det_count = det_fields.shape[0]
    groups = lax.axis_size("blk")
    det_total = det_count * groups
    probe_count = probes.shape[0]
    weighted = (src_fields.astype(jnp.float32)[None] * probes.astype(jnp.float32)[:, None]).astype(
        jnp.bfloat16
    )
    weighted = weighted.reshape(probe_count * src_count, vox_count)
    portion = lax.all_gather(det_fields, "blk", axis=0, tiled=True)
    slab = portion
    product = jnp.einsum("rv,dv->rd", weighted, portion, preferred_element_type=jnp.float32)
    partial_value, slab = (product, slab)
    measured = total_of(partial_value, "vox")
    measured_b = measured.astype(jnp.bfloat16)
    backproj = jnp.dot(measured_b, slab, preferred_element_type=jnp.float32)
    backproj = backproj.reshape(probe_count, src_count, vox_count)
    contrib = jnp.sum(src_fields.astype(jnp.float32)[None] * backproj, axis=1)
    total = of_everyone(contrib, "blk")
    normalizer = jnp.float32(1.0 / (src_count * groups * det_total))
    return total * normalizer


def solution(mesh):
    return jax.shard_map(
        shards,
        mesh=mesh,
        in_specs=(P("blk", "vox"), P("blk", "vox"), P(None, "vox")),
        out_specs=P(None, "vox"),
        check_vma=False,
    )
```

profile of v0, /device:TPU:1, one launch (start us, length us, event | category | flops | bytes accessed | tf_op | source)
XLA Modules:
  0.0 211.5 jit_solution(65355358344800486)
XLA Ops:
  6.5 0.0 all-gather.2.cloned.1.call-start
  6.5 0.7 all-gather.2.cloned.1.call-update
  7.3 2.6 %mul.33 = f32[2,64,4096]{2,1,0:T(8,128)} broadcast(bf16[64,4096]{1,0:T(8,128)(2,1)} %param.3), dimensions={1,2} | broadcast | bytes 2621440 | tf_op jit(solution)/shard_map/mul | solution.py:71
  9.9 0.0 copy-start.1
  9.9 1.9 mul.34
  11.8 92.7 %all-gather.2.cloned.1.call-done = bf16[1024,4096]{1,0:T(8,128)(2,1)} async-done(((bf16[64,4096]{1,0:T(8,128)(2,1)}), bf16[1024,4096]{1,0:T(8,128)(2,1)}) %all-gather.2.cloned.1.call-update) | async-done | bytes 8388624 | tf_op jit(solution)/shard_map/all_gather | solution.py:63
  104.5 0.0 copy-done.1
  104.5 6.6 %fusion.2 = f32[32,4,1024]{2,0,1:T(8,128)S(1)} fusion(bf16[1024,4096]{1,0:T(8,128)(2,1)} %all-gather.2.cloned.1.call-done, f32[32,4,4096]{2,1,0:T(4,128)S(1)} %mul.34, f32[32,4096]{1,0:T(8,128)S(1)} %bitcast.11), kind=kOutput, calls=%fused_computation.2 | convolution fusion | flops 1074790400 | bytes 11534336 | tf_op jit(solution)/shard_map/rv,dv->rd/dot_general | solution.py:65
  111.1 0.0 copy-start
  111.2 0.3 copy.10
  111.5 44.3 %all_to_all.15 = f32[32,4,1024]{2,1,0:T(4,128)S(1)} all-to-all(f32[32,4,1024]{2,1,0:T(4,128)S(1)} %copy.10), channel_id=1, replica_groups=mesh['blk'=16,'vox'=32] {'vox'}, dimensions={0} | all-to-all | bytes 1048576 | tf_op jit(solution)/shard_map/all_to_all | solution.py:37
  155.8 0.1 reduce_sum.27
  155.9 0.8 broadcast_in_dim.4
  156.7 4.2 %all-to-all-start.1 = ((bf16[32,4,1024]{2,1,0:T(4,128)(2,1)}), bf16[32,4,1024]{2,1,0:T(4,128)(2,1)S(1)}, u32[]{:S(2)}, u32[]{:S(2)}) async-start(bf16[32,4,1024]{2,1,0:T(4,128)(2,1)} %broadcast_in_dim.4), calls=%async_computation.1 | async-start | bytes 524288 | tf_op jit(solution)/shard_map/all_to_all | solution.py:16
  160.9 0.0 copy-done
  161.0 0.1 convert_element_type.19
  161.0 19.7 %all-to-all-done.1 = bf16[32,4,1024]{2,1,0:T(4,128)(2,1)S(1)} async-done(((bf16[32,4,1024]{2,1,0:T(4,128)(2,1)}), bf16[32,4,1024]{2,1,0:T(4,128)(2,1)S(1)}, u32[]{:S(2)}, u32[]{:S(2)}) %all-to-all-start.1) | async-done | bytes 262176 | tf_op jit(solution)/shard_map/all_to_all | solution.py:16
  180.8 0.1 convert_element_type.23
  180.8 4.7 %fusion.8 = f32[2,4096]{1,0:T(2,128)S(1)} fusion(bf16[2,64,1024]{2,1,0:T(8,128)(2,1)S(1)} %convert_element_type.23, bf16[1024,4096]{1,0:T(8,128)(2,1)} %all-gather.2.cloned.1.call-done, f32[64,4096]{1,0:T(8,128)S(1)} %convert_element_type.19), kind=kOutput, calls=%fused_computation.7 | convolution fusion | flops 1074782208 | bytes 9732096 | tf_op jit(solution)/shard_map/dot_general | solution.py:69
  185.6 0.2 broadcast_in_dim.10
  185.8 18.1 %all_to_all.16 = f32[16,2,4096]{2,1,0:T(2,128)S(1)} all-to-all(f32[16,2,4096]{2,1,0:T(2,128)S(1)} %broadcast_in_dim.10), channel_id=1, replica_groups=mesh['blk'=16,'vox'=32] {'blk'}, dimensions={0} | all-to-all | bytes 1048576 | tf_op jit(solution)/shard_map/all_to_all | solution.py:16
  203.9 0.2 reduce_sum.29
  204.1 0.6 broadcast_multiply_fusion
  (1 shorter events, 0.0 us)
Async XLA Ops:
  6.5 98.0 %all-gather.2.cloned.1.call-start = ((), (), s32[]{:S(2)}) async-start(), calls=%async_computation.3 | async-start | bytes 8912896 | tf_op jit(solution)/shard_map/all_gather | solution.py:63
  9.9 94.6 %copy-start.1 = (bf16[2,4096]{1,0:T(2,128)(2,1)S(1)}, bf16[2,4096]{1,0:T(2,128)(2,1)}, u32[]{:S(2)}) copy-start(bf16[2,4096]{1,0:T(2,128)(2,1)} %param.5) | copy-start | bytes 49156
  111.1 49.8 %copy-start = (bf16[64,4096]{1,0:T(8,128)(2,1)S(1)}, bf16[64,4096]{1,0:T(8,128)(2,1)}, u32[]{:S(2)}) copy-start(bf16[64,4096]{1,0:T(8,128)(2,1)} %param.3) | copy-start | bytes 1572868
  156.7 24.1 %all-to-all-start.1 = ((bf16[32,4,1024]{2,1,0:T(4,128)(2,1)}), bf16[32,4,1024]{2,1,0:T(4,128)(2,1)S(1)}, u32[]{:S(2)}, u32[]{:S(2)}) async-start(bf16[32,4,1024]{2,1,0:T(4,128)(2,1)} %broadcast_in_dim.4), calls=%async_computation.1 | async-start | bytes 524288 | tf_op jit(solution)/shard_map/all_to_all | solution.py:16
Sparse Core Ops, SparseCore 0:
  10.6 93.8 all-gather.1
where the time goes:
time: 212 us
  waiting for transfers between devices  113 us (53%)
  blocking collectives  62.5 us (29%)
  between operations  13.5 us (6%)
  matrix products  11.3 us (5%)
  local copies, waits for them, and re-layouts  5.94 us (3%)
  starting transfers between devices  4.23 us (2%)
    all_gather x1, waiting for transfers between devices, shards(): portion = lax.all_gather(det_fields, 'blk', axis=0, tiled=True)  92.7 us
    all_to_all x1, blocking collectives, summed_on_arrival(): tiles = lax.all_to_all(cut_along(value, dim, count), axis, 0, 0, tiled=True)  44.3 us
    all_to_all x1, waiting for transfers between devices, from_everyone(): return lax.all_to_all(copies, axis, split_axis=0, concat_axis=0, tiled=True)  19.7 us
    all_to_all x1, blocking collectives, from_everyone(): return lax.all_to_all(copies, axis, split_axis=0, concat_axis=0, tiled=True)  18.1 us
    dot_general x1, matrix products, shards(): jnp.einsum('rv,dv->rd', weighted, portion, preferred_element_type=jnp.flo...  6.6 us
    dot_general x1, matrix products, shards(): backproj = jnp.dot(measured_b, slab, preferred_element_type=jnp.float32)  4.71 us
    mul x2, local copies, waits for them, and re-layouts, shards(): contrib = jnp.sum(src_fields.astype(jnp.float32)[None] * backproj, axis=1)  4.52 us
  transfers between devices with their start and end apart: 2, of which 2 were waited for; matrix products, arithmetic and copies ran while one was open for 2% of the time, Pallas kernels for 0%

commit v1 on v0

v1 whole, which is shorter than its diff:
```python
import functools

import jax
import jax.numpy as jnp
from jax import lax
from jax.experimental import pallas as pl
from jax.experimental.pallas import tpu as pltpu
from jax.sharding import PartitionSpec as P

MESH = pl.DeviceIdType.MESH
BF16 = jnp.bfloat16
F32 = jnp.float32
DMA = pltpu.SemaphoreType.DMA

NX, NY, NZ, NC = 4, 4, 16, 2
NQ = 8


def device(x, y, z, c):
    return (x * 4 + (y // 2) * 2 + c, z * 2 + y % 2)


def send(src, dst, send_sem, recv_sem, to):
    pltpu.make_async_remote_copy(
        src_ref=src, dst_ref=dst, send_sem=send_sem, recv_sem=recv_sem, device_id=to, device_id_type=MESH
    ).start()


def wait_for(ref, sem):
    pltpu.make_async_copy(ref, ref, sem).wait()


def kernel(
    scale,
    src_hbm,
    det_hbm,
    probes_hbm,
    out,
    src_v,
    det_v,
    pr_v,
    pr_in,
    pr_f,
    S,
    D,
    acc,
    tx1P,
    tx1Q,
    rx1P,
    rx1Q,
    tx2P,
    tx2Q,
    rx2P,
    rx2Q,
    zs,
    zr,
    mz,
    MP,
    MQ,
    cv,
    cr,
    fin,
    ob,
    ld,
    ysend,
    yS,
    yD,
    xsend,
    xS,
    xD,
    c0,
    c1,
    r1send,
    r1P,
    r1Q,
    r2send,
    r2P,
    r2Q,
    zsend,
    zrecv,
    gsend,
    grecv,
    asend,
    aP,
    aQ,
    bsend,
    bP,
    bQ,
    csend,
    crecv,
    fsend,
    frecv,
):
    blk = lax.axis_index("blk")
    vox = lax.axis_index("vox")
    x, yh, c = blk // 4, (blk // 2) % 2, blk % 2
    z, yl = vox // 2, vox % 2
    y = yh * 2 + yl
    half = src_v.shape[1] // 2
    vc = half // NQ

    up, down = (y + 1) % NY, (y + 3) % NY
    u, v = (yh + yl) % 2, yh
    ya, yb = yh * 2 + 1 - yl, 3 - y
    xs = (x // 2) * 2 + 1 - x % 2
    xd = 3 - x
    zg, zt = z // 4, z % 4

    dev_up, dev_down = device(x, up, z, c), device(x, down, z, c)
    dev_a, dev_b = device(x, ya, z, c), device(x, yb, z, c)
    dev_xs, dev_xd = device(xs, y, z, c), device(xd, y, z, c)
    dev_c = device(x, y, z, 1 - c)
    me = x * 2 + c

    pltpu.make_async_copy(det_hbm, det_v, ld.at[0]).start()
    pltpu.make_async_copy(src_hbm, src_v, ld.at[1]).start()
    pltpu.make_async_copy(probes_hbm, pr_v, ld.at[2]).start()

    barrier = pltpu.get_barrier_semaphore()

    def greet_z(j, carry):
        pl.semaphore_signal(barrier, inc=1, device_id=device(x, y, (z + j) % NZ, c), device_id_type=MESH)
        return carry

    lax.fori_loop(1, NZ, greet_z, 0)

    def greet_plane(j, carry):
        e = (me + j) % NQ
        pl.semaphore_signal(barrier, inc=1, device_id=device(e // 2, y, z, e % 2), device_id_type=MESH)
        return carry

    lax.fori_loop(1, NQ, greet_plane, 0)

    def greet_rows(e, carry):
        pl.semaphore_signal(barrier, inc=1, device_id=device(e // 2, up, z, e % 2), device_id_type=MESH)
        pl.semaphore_signal(barrier, inc=1, device_id=device(e // 2, down, z, e % 2), device_id_type=MESH)
        return carry

    lax.fori_loop(0, NQ, greet_rows, 0)
    pl.semaphore_wait(barrier, NZ - 1 + NQ - 1 + 2 * NQ)

    h_up, h_down = up // 2, down // 2
    mine = pl.ds(pl.multiple_of(yh * 64, 64), 64)
    wait_for(det_v, ld.at[0])
    wait_for(src_v, ld.at[1])
    wait_for(pr_v, ld.at[2])
    send(
        pr_v.at[:, pl.ds(pl.multiple_of(h_up * half, half), half)],
        pr_in,
        ysend.at[2],
        ysend.at[3],
        dev_up,
    )

    def spread(q, carry):
        to_up = pl.ds(pl.multiple_of(h_up * half + q * vc, vc), vc)
        to_down = pl.ds(pl.multiple_of(h_down * half + q * vc, vc), vc)
        send(det_v.at[:, to_up], D.at[q, mine], ysend.at[0], yD.at[q], dev_up)
        send(det_v.at[:, to_down], D.at[q, mine], ysend.at[0], yD.at[q], dev_down)
        send(src_v.at[:, to_up], S.at[q, mine], ysend.at[1], yS.at[q], dev_up)
        send(src_v.at[:, to_down], S.at[q, mine], ysend.at[1], yS.at[q], dev_down)
        return carry

    lax.fori_loop(0, NQ, spread, 0)

    acc[...] = jnp.zeros_like(acc)
    wait_for(pr_in, ysend.at[3])
    for q in range(NQ):
        pr_f[q] = pr_in[:, q * vc : (q + 1) * vc].astype(F32)

    own, other = pl.ds(0, 128), pl.ds(128, 128)

    def pass_own(q):
        wait_for(D.at[q, own], yD.at[q])
        send(D.at[q, own], D.at[q, other], xsend.at[1], xD.at[q], dev_xd)
        send(D.at[q, own], D.at[q, pl.ds(256, 128)], xsend.at[2], c0.at[q], dev_c)
        wait_for(S.at[q, own], yS.at[q])
        send(S.at[q, own], S.at[q, other], xsend.at[0], xS.at[q], dev_xs)

    def pass_other(q):
        wait_for(D.at[q, other], xD.at[q])
        send(D.at[q, other], D.at[q, pl.ds(384, 128)], xsend.at[3], c1.at[q], dev_c)

    def measure(q):
        wait_for(S.at[q, other], xS.at[q])
        wait_for(D.at[q, pl.ds(256, 128)], c0.at[q])
        wait_for(D.at[q, pl.ds(384, 128)], c1.at[q])
        fields = S[q].astype(F32)
        p = pr_f[q]
        det = D[q]
        for k in range(2):
            weighted = (fields * p[k : k + 1]).astype(BF16)
            part = lax.dot_general(weighted, det, (((1,), (1,)), ((), ())), preferred_element_type=F32)
            for g in range(4):
                acc[g, k] += part[:, g * 128 : (g + 1) * 128].reshape(2, 2, 64, 128)

    pass_own(0)
    pass_own(1)
    pass_other(0)

    def gather(q, carry):
        pass_own(q)
        pass_other(q - 1)
        measure(q - 2)
        return carry

    lax.fori_loop(2, NQ, gather, 0)
    pass_other(NQ - 1)
    measure(NQ - 2)
    measure(NQ - 1)

    groups = [(zg + o) % 4 for o in (2, 1, 3, 0)]
    for i, g in enumerate(groups):
        tx1P[i] = acc[g, 0, 1 - u].astype(BF16)
        send(tx1P.at[i], rx1P.at[i], r1send.at[0], r1P.at[i], dev_a)
        tx1Q[i, 0] = acc[g, 1, 0, 1 - v].astype(BF16)
        tx1Q[i, 1] = acc[g, 1, 1, 1 - v].astype(BF16)
        send(tx1Q.at[i], rx1Q.at[i], r1send.at[1], r1Q.at[i], dev_b)

    def second(i):
        g = groups[i]
        wait_for(rx1P.at[i], r1P.at[i])
        tx2P[i] = (acc[g, 0, u, 1 - v] + rx1P[i, 1 - v].astype(F32)).astype(BF16)
        send(tx2P.at[i], rx2P.at[i], r2send.at[0], r2P.at[i], dev_b)
        wait_for(rx1Q.at[i], r1Q.at[i])
        tx2Q[i] = (acc[g, 1, 1 - u, v] + rx1Q[i, 1 - u].astype(F32)).astype(BF16)
        send(tx2Q.at[i], rx2Q.at[i], r2send.at[1], r2Q.at[i], dev_a)
        acc[g, 0, u, v] += rx1P[i, v].astype(F32)
        acc[g, 1, u, v] += rx1Q[i, u].astype(F32)

    def third(i):
        g = groups[i]
        wait_for(rx2P.at[i], r2P.at[i])
        zs[i, :, 0] = (acc[g, 0, u, v] + rx2P[i].astype(F32)).reshape(4, 16, 128).astype(BF16)
        wait_for(rx2Q.at[i], r2Q.at[i])
        zs[i, :, 1] = (acc[g, 1, u, v] + rx2Q[i].astype(F32)).reshape(4, 16, 128).astype(BF16)
        for j in range(4):
            t = (zt + 4 - j) % 4
            if i == 3 and j == 0:
                continue
            send(zs.at[i, t], zr.at[z], zsend, zrecv, device(x, y, g * 4 + t, c))

    second(0)
    second(1)
    third(0)
    second(2)
    third(1)
    second(3)
    third(2)
    third(3)
    zr[z] = zs[3, zt]
    wait_for(zr.at[pl.ds(0, NZ - 1)], zrecv)
    total = zr[0].astype(F32)
    for j in range(1, NZ):
        total += zr[j].astype(F32)
    mz[...] = total.astype(BF16)

    MP[zg, u, v, zt] = mz[0]
    MQ[zg, u, v, zt] = mz[1]
    for j in range(NZ - 1):
        step = NZ // 2 + ((j + 1) // 2) * (1 if j % 2 else -1)
        to = device(x, y, (z + step) % NZ, c)
        send(mz.at[0], MP.at[zg, u, v, zt], gsend, grecv.at[zg], to)
        send(mz.at[1], MQ.at[zg, u, v, zt], gsend, grecv.at[zg], to)

    back = [(zg + o) % 4 for o in (0, 1, 3, 2)]

    def first_back(i):
        g = back[i]
        wait_for(zr.at[pl.ds(0, 4 if i else 3)], grecv.at[g])
        send(MP.at[g, u, v], MP.at[g, u, v], asend.at[0], aP.at[g], dev_b)
        send(MQ.at[g, u, v], MQ.at[g, u, v], asend.at[1], aQ.at[g], dev_a)

    def second_back(i):
        g = back[i]
        wait_for(MP.at[g, u, 1 - v], aP.at[g])
        send(MP.at[g, u], MP.at[g, u], bsend.at[0], bP.at[g], dev_a)
        wait_for(MQ.at[g, 1 - u, v], aQ.at[g])
        send(MQ.at[g, 0, v], MQ.at[g, 0, v], bsend.at[1], bQ.at[g], dev_b)
        send(MQ.at[g, 1, v], MQ.at[g, 1, v], bsend.at[1], bQ.at[g], dev_b)

    def third_back(i):
        g = back[i]
        wait_for(MP.at[g, 1 - u], bP.at[g])
        wait_for(MQ.at[g, 1 - u], bQ.at[g])

    def contribution(q, lo):
        g0, g1 = back[lo], back[lo + 1]
        det = jnp.concatenate(
            [
                D[q, pl.ds(pl.multiple_of(g0 * 128, 128), 128)],
                D[q, pl.ds(pl.multiple_of(g1 * 128, 128), 128)],
            ],
            axis=0,
        )
        fields = S[q].astype(F32)
        rows = []
        for m in (MP, MQ):
            lhs = jnp.concatenate([m[g0].reshape(256, 128), m[g1].reshape(256, 128)], axis=1)
            bp = jnp.dot(lhs, det, preferred_element_type=F32)
            rows.append(jnp.sum(fields * bp, axis=0, keepdims=True))
        return jnp.concatenate(rows, axis=0)

    first_back(0)
    first_back(1)
    second_back(0)
    first_back(2)
    second_back(1)
    first_back(3)
    third_back(0)
    third_back(1)

    second_back(2)

    def front(q, carry):
        cv[q] = contribution(q, 0)
        return carry

    lax.fori_loop(0, NQ, front, 0)
    second_back(3)
    third_back(2)
    third_back(3)

    def rest(j, carry):
        q = (me + j) % NQ
        cv[q] = cv[q] + contribution(q, 2)
        send(cv.at[q], cr.at[me], csend, crecv, device(q // 2, y, z, q % 2))
        return carry

    lax.fori_loop(1, NQ, rest, 0)
    cr[me] = cv[me] + contribution(me, 2)
    wait_for(cr.at[pl.ds(0, NQ - 1)], crecv)
    whole = cr[0]
    for j in range(1, NQ):
        whole += cr[j]
    fin[...] = whole * scale

    def hand_out(e, carry):
        send(fin, ob.at[yh, me], fsend, frecv, device(e // 2, up, z, e % 2))
        send(fin, ob.at[yh, me], fsend, frecv, device(e // 2, down, z, e % 2))
        return carry

    lax.fori_loop(0, NQ, hand_out, 0)

    wait_for(det_v, ysend.at[0])
    wait_for(src_v, ysend.at[1])
    wait_for(pr_in, ysend.at[2])
    wait_for(S.at[:, own], xsend.at[0])
    wait_for(D.at[:, own], xsend.at[1])
    wait_for(D.at[:, own], xsend.at[2])
    wait_for(D.at[:, own], xsend.at[3])
    wait_for(tx1P, r1send.at[0])
    wait_for(tx1Q, r1send.at[1])
    wait_for(tx2P, r2send.at[0])
    wait_for(tx2Q, r2send.at[1])
    wait_for(zr.at[pl.ds(0, NZ - 1)], zsend)
    wait_for(zr.at[pl.ds(0, NZ - 1)], gsend)
    wait_for(tx2P, asend.at[0])
    wait_for(tx2P, asend.at[1])
    wait_for(tx1P, bsend.at[0])
    wait_for(tx1P, bsend.at[1])
    wait_for(cr.at[pl.ds(0, NQ - 1)], csend)
    wait_for(ob, frecv)
    for h in range(2):
        for e in range(NQ):
            at = h * half + e * vc
            out[:, at : at + vc] = ob[h, e]
    wait_for(ob, fsend)


def shards(src_fields, det_fields, probes):
    rows, voxels = src_fields.shape
    half = voxels // 2
    vc = half // NQ
    sources, detectors = rows * lax.axis_size("blk"), det_fields.shape[0] * lax.axis_size("blk")
    scale = 1.0 / (sources * detectors)
    any_spec = pl.BlockSpec(memory_space=pl.ANY)
    return pl.pallas_call(
        functools.partial(kernel, scale),
        out_shape=jax.ShapeDtypeStruct((2, voxels), F32),
        in_specs=[any_spec] * 3,
        out_specs=pl.BlockSpec(memory_space=pltpu.VMEM),
        scratch_shapes=[
            pltpu.VMEM((64, voxels), BF16),
            pltpu.VMEM((64, voxels), BF16),
            pltpu.VMEM((2, voxels), BF16),
            pltpu.VMEM((2, half), BF16),
            pltpu.VMEM((NQ, 2, vc), F32),
            pltpu.VMEM((NQ, 256, vc), BF16),
            pltpu.VMEM((NQ, 512, vc), BF16),
            pltpu.VMEM((4, 2, 2, 2, 64, 128), F32),
            pltpu.VMEM((4, 2, 64, 128), BF16),
            pltpu.VMEM((4, 2, 64, 128), BF16),
            pltpu.VMEM((4, 2, 64, 128), BF16),
            pltpu.VMEM((4, 2, 64, 128), BF16),
            pltpu.VMEM((4, 64, 128), BF16),
            pltpu.VMEM((4, 64, 128), BF16),
            pltpu.VMEM((4, 64, 128), BF16),
            pltpu.VMEM((4, 64, 128), BF16),
            pltpu.VMEM((4, 4, 2, 16, 128), BF16),
            pltpu.VMEM((NZ, 2, 16, 128), BF16),
            pltpu.VMEM((2, 16, 128), BF16),
            pltpu.VMEM((4, 2, 2, 4, 16, 128), BF16),
            pltpu.VMEM((4, 2, 2, 4, 16, 128), BF16),
            pltpu.VMEM((NQ, 2, vc), F32),
            pltpu.VMEM((NQ, 2, vc), F32),
            pltpu.VMEM((2, vc), F32),
            pltpu.VMEM((2, NQ, 2, vc), F32),
            DMA((3,)),
            DMA((4,)),
            DMA((NQ,)),
            DMA((NQ,)),
            DMA((4,)),
            DMA((NQ,)),
            DMA((NQ,)),
            DMA((NQ,)),
            DMA((NQ,)),
            DMA((2,)),
            DMA((4,)),
            DMA((4,)),
            DMA((2,)),
            DMA((4,)),
            DMA((4,)),
            DMA,
            DMA,
            DMA,
            DMA((4,)),
            DMA((2,)),
            DMA((4,)),
            DMA((4,)),
            DMA((2,)),
            DMA((4,)),
            DMA((4,)),
            DMA,
            DMA,
            DMA,
            DMA,
        ],
        compiler_params=pltpu.CompilerParams(collective_id=0, has_side_effects=True),
        name="gauss_newton",
    )(src_fields, det_fields, probes)


def solution(mesh):
    return jax.shard_map(
        shards,
        mesh=mesh,
        in_specs=(P("blk", "vox"), P("blk", "vox"), P(None, "vox")),
        out_specs=P(None, "vox"),
        check_vma=False,
    )
```

time: 212 us -> 89.7 us (0.42)
  waiting for transfers between devices: 113 us -> 0 us
  Pallas kernels: 0 us -> 88.1 us
  blocking collectives: 62.5 us -> 0 us
  between operations: 13.5 us -> 0.01 us
  matrix products: 11.3 us -> 0 us
  local copies, waits for them, and re-layouts: 5.94 us -> 1.38 us
  starting transfers between devices: 4.23 us -> 0 us
    all_gather x1 -> x0, waiting for transfers between devices: 92.7 us -> none  [shards(): portion = lax.all_gather(det_fields, 'blk', axis=0, tiled=True)]
    pallas_call x0 -> x1, Pallas kernels: none -> 88.1 us  [shards(): pl.pallas_call(functools.partial(kernel, scale), out_shape=jax.ShapeDtype...]
    all_to_all x2 -> x0, blocking collectives: 62.5 us -> none  [the longest x1 44.3 us: summed_on_arrival(): tiles = lax.all_to_all(cut_along(value, dim, count), axis, 0, 0, tiled=True)]
    all_to_all x1 -> x0, waiting for transfers between devices: 19.7 us -> none  [from_everyone(): return lax.all_to_all(copies, axis, split_axis=0, concat_axis=0, tiled=True)]
    dot_general x2 -> x0, matrix products: 11.3 us -> none  [the longest x1 6.6 us: shards(): jnp.einsum('rv,dv->rd', weighted, portion, preferred_element_type=jnp.flo...]
    mul x3 -> x0, local copies, waits for them, and re-layouts: 4.55 us -> none  [the longest x2 4.52 us: shards(): contrib = jnp.sum(src_fields.astype(jnp.float32)[None] * backproj, axis=1)]
    all_to_all x1 -> x0, starting transfers between devices: 4.23 us -> none  [from_everyone(): return lax.all_to_all(copies, axis, split_axis=0, concat_axis=0, tiled=True)]
  transfers between devices with their start and end apart: 2 -> 0, of which waited for: 2 -> 0; matrix products, arithmetic and copies ran while one was open for 2% -> 0% of each run, Pallas kernels for 0% -> 0%
where the time goes in v1:
time: 89.7 us; the launch traced here: 89.5 us
  Pallas kernels  88.1 us (98%)
  local copies, waits for them, and re-layouts  1.38 us (2%)
    pallas_call x1, Pallas kernels, shards(): pl.pallas_call(functools.partial(kernel, scale), out_shape=jax.ShapeDtype...  88.1 us

profile of v1, /device:TPU:1, one launch (start us, length us, event | category | flops | bytes accessed | tf_op | source)
XLA Modules:
  0.0 89.5 jit_solution(10742552437817724232)
XLA Ops:
  0.0 88.1 %gauss_newton.1 = f32[2,4096]{1,0:T(2,128)} custom-call(bf16[64,4096]{1,0:T(8,128)(2,1)} %src_hbm.1, bf16[64,4096]{1,0:T(8,128)(2,1)} %det_hbm.1, bf16[2,4096]{1,0:T(2,128)(2,1)} %probes_hbm.1), custom_call_target="tpu_custom_call" | custom-call | tf_op jit(solution)/shard_map/gauss_newton/pallas_call | solution.py:378
  88.1 1.4 %copy.5 = f32[2,4096]{1,0:T(2,128)} copy(f32[2,4096]{1,0:T(2,128)} %gauss_newton.1) | data formatting | bytes 65536

commit v2 on v0

v2 whole, which is shorter than its diff:
```python
import functools

import jax
import jax.numpy as jnp
from jax import lax
from jax.experimental import pallas as pl
from jax.experimental.pallas import tpu as pltpu
from jax.sharding import PartitionSpec as P

MESH = pl.DeviceIdType.MESH
BF16 = jnp.bfloat16
F32 = jnp.float32
DMA = pltpu.SemaphoreType.DMA

NX, NY, NZ, NC = 4, 4, 16, 2
NQ = 8
NB = 4


def device(x, y, z, c):
    return (x * 4 + (y // 2) * 2 + c, z * 2 + y % 2)


def send(src, dst, send_sem, recv_sem, to):
    pltpu.make_async_remote_copy(
        src_ref=src, dst_ref=dst, send_sem=send_sem, recv_sem=recv_sem, device_id=to, device_id_type=MESH
    ).start()


def wait_for(ref, sem):
    pltpu.make_async_copy(ref, ref, sem).wait()


def kernel(
    scale,
    src_hbm,
    det_hbm,
    probes_hbm,
    out,
    src_v,
    det_v,
    pr_v,
    pr_in,
    S,
    D,
    acc,
    tx,
    rx,
    zs,
    zr,
    mz,
    M,
    part,
    cv,
    ob,
    ld,
    ysend,
    yS,
    yD,
    pS,
    xsend,
    xS,
    xD,
    c0,
    c1,
    rsend,
    rrecv,
    zsend,
    zrecv,
    gsend,
    grecv,
    asend,
    arecv,
    fsend,
    frecv,
    ready,
):
    blk = lax.axis_index("blk")
    vox = lax.axis_index("vox")
    x, yh, c = blk // 4, (blk // 2) % 2, blk % 2
    z, yl = vox // 2, vox % 2
    y = yh * 2 + yl
    half = src_v.shape[1] // 2
    vc = half // NQ
    scope = jax.named_scope

    up, down = (y + 1) % NY, (y + 3) % NY
    xs = (x // 2) * 2 + 1 - x % 2
    xd = 3 - x
    zg, zt = z // 4, z % 4
    me = x * 2 + c
    dev_up, dev_down = device(x, up, z, c), device(x, down, z, c)
    dev_xs, dev_xd = device(xs, y, z, c), device(xd, y, z, c)
    dev_c = device(x, y, z, 1 - c)

    def dev_z(d):
        return device(x, y, (z + NZ + d) % NZ, c)

    def signal(sem, to):
        pl.semaphore_signal(sem, inc=1, device_id=to, device_id_type=MESH)

    barrier = pltpu.get_barrier_semaphore()
    near = (dev_up, dev_down, dev_xs, dev_xd, dev_c, dev_z(1), dev_z(-1))
    for to in near:
        signal(barrier, to)

    h_up, h_down = up // 2, down // 2

    def columns(h, q):
        return pl.ds(pl.multiple_of(h * half + q * vc, vc), vc)

    pltpu.make_async_copy(probes_hbm, pr_v, ld.at[NQ]).start()
    for q in range(NQ):
        for h in range(2):
            at = pl.ds(h * half + q * vc, vc)
            pltpu.make_async_copy(det_hbm.at[:, at], det_v.at[:, at], ld.at[q]).start()
            pltpu.make_async_copy(src_hbm.at[:, at], src_v.at[:, at], ld.at[q]).start()
    with scope("t_barrier"):
        pl.semaphore_wait(barrier, len(near))

    def spread_word(r):
        d = 2**r
        if r:
            pl.semaphore_wait(ready.at[r - 1], 2)
        if r < 3:
            signal(ready.at[r], dev_z(d))
            signal(ready.at[r], dev_z(-d))

    mine = pl.ds(pl.multiple_of(yh * 64, 64), 64)
    own, other = pl.ds(0, 128), pl.ds(128, 128)
    for q in range(NQ):
        with scope("t_load%d" % q):
            wait_for(D.at[q, pl.ds(0, 256)], ld.at[q])
        send(det_v.at[:, columns(h_up, q)], D.at[q, mine], ysend.at[0], yD.at[q], dev_up)
        send(det_v.at[:, columns(h_down, q)], D.at[q, mine], ysend.at[0], yD.at[q], dev_down)
        send(src_v.at[:, columns(h_up, q)], S.at[q, mine], ysend.at[1], yS.at[q], dev_up)
        send(src_v.at[:, columns(h_down, q)], S.at[q, mine], ysend.at[1], yS.at[q], dev_down)
        if q == 0:
            wait_for(pr_v, ld.at[NQ])
            send(
                pr_v.at[:, pl.ds(pl.multiple_of(h_up * half, half), half)],
                pr_in,
                ysend.at[2],
                pS,
                dev_up,
            )
            spread_word(0)

    def pass_own(q):
        wait_for(D.at[q, own], yD.at[q])
        send(D.at[q, own], D.at[q, other], xsend.at[1], xD.at[q], dev_xd)
        send(D.at[q, own], D.at[q, pl.ds(256, 128)], xsend.at[2], c0.at[q], dev_c)
        wait_for(S.at[q, own], yS.at[q])
        send(S.at[q, own], S.at[q, other], xsend.at[0], xS.at[q], dev_xs)

    def pass_other(q):
        wait_for(D.at[q, other], xD.at[q])
        send(D.at[q, other], D.at[q, pl.ds(384, 128)], xsend.at[3], c1.at[q], dev_c)

    def measure(q):
        wait_for(S.at[q, other], xS.at[q])
        wait_for(D.at[q, pl.ds(256, 128)], c0.at[q])
        wait_for(D.at[q, pl.ds(384, 128)], c1.at[q])
        fields = S[q].astype(F32)
        p = pr_in[:, q * vc : (q + 1) * vc].astype(F32)
        det = D[q]
        for k in range(2):
            weighted = (fields * p[k : k + 1]).astype(BF16)
            sums = lax.dot_general(weighted, det, (((1,), (1,)), ((), ())), preferred_element_type=F32)
            for g in range(4):
                piece = sums[:, g * 128 : (g + 1) * 128].reshape(4, 64, 128)
                if q:
                    acc[g, :, k] += piece
                else:
                    acc[g, :, k] = piece

    word = {1: 1, 4: 2, 7: 3}
    for t in range(NQ + 4):
        if t < NQ:
            with scope("g%02d_own" % t):
                pass_own(t)
        if t in word:
            with scope("g%02d_word" % t):
                spread_word(word[t])
        if 0 <= t - 3 < NQ:
            with scope("g%02d_other" % t):
                pass_other(t - 3)
        if t == 4:
            wait_for(pr_in, pS)
        if 0 <= t - 4 < NQ:
            with scope("g%02d_meas" % t):
                measure(t - 4)

    groups = [(zg + o) % 4 for o in (2, 1, 3, 0)]
    for i, g in enumerate(groups):
        for d in (2, 1, 3):
            to = (y + d) % NY
            tx[i, to] = acc[g, to].astype(BF16)
            send(tx.at[i, to], rx.at[i, y], rsend, rrecv.at[i], device(x, to, z, c))

    for i, g in enumerate(groups):
        with scope("r%d_y" % i):
            wait_for(rx.at[i, pl.ds(0, 3)], rrecv.at[i])
        total = acc[g, y]
        for d in (1, 2, 3):
            total += rx[i, (y + d) % NY].astype(F32)
        total = total.astype(BF16)
        for k in range(2):
            zs[i, :, k] = total[k].reshape(4, 16, 128)
        for j in range(4):
            t = (zt + 4 - j) % 4
            if i == 3 and j == 0:
                continue
            send(zs.at[i, t], zr.at[z], zsend, zrecv, device(x, y, g * 4 + t, c))
    zr[z] = zs[3, zt]
    with scope("r_z"):
        wait_for(zr.at[pl.ds(0, NZ - 1)], zrecv)
    total = zr[0].astype(F32)
    for j in range(1, NZ):
        total += zr[j].astype(F32)
    mz[...] = total.astype(BF16)

    M[zg, y, zt] = mz[...]
    for j in range(NZ - 1):
        step = NZ // 2 + ((j + 1) // 2) * (1 if j % 2 else -1)
        send(mz, M.at[zg, y, zt], gsend, grecv.at[zg], dev_z(step))

    back = [(zg + o) % 4 for o in (0, 1, 3, 2)]
    for i, g in enumerate(back):
        with scope("b%d_z" % i):
            wait_for(zr.at[pl.ds(0, 4 if i else 3)], grecv.at[g])
        for d in (2, 1, 3):
            send(M.at[g, y], M.at[g, y], asend, arecv.at[g], device(x, (y + d) % NY, z, c))

    def contribution(q, lo):
        lhs = jnp.concatenate([M[back[i]].reshape(512, 128) for i in (lo, lo + 1)], axis=1)
        det = jnp.concatenate(
            [D[q, pl.ds(pl.multiple_of(back[i] * 128, 128), 128)] for i in (lo, lo + 1)], axis=0
        )
        bp = jnp.dot(lhs, det, preferred_element_type=F32).reshape(16, 2, 16, vc)
        fields = S[q].astype(F32).reshape(16, 16, vc)
        rows = [jnp.sum(jnp.sum(fields * bp[:, k], axis=0), axis=0, keepdims=True) for k in range(2)]
        return jnp.concatenate(rows, axis=0)

    for i in range(2):
        with scope("b%d_y" % i):
            wait_for(M.at[back[i], pl.ds(0, 3)], arecv.at[back[i]])
    with scope("m_front"):
        for q in range(NQ):
            part[q] = contribution(q, 0)
    for i in range(2, 4):
        with scope("b%d_y" % i):
            wait_for(M.at[back[i], pl.ds(0, 3)], arecv.at[back[i]])

    per = NQ // NB
    with scope("m_rest"):
        for b in range(NB):
            for a in range(per):
                q = b * per + a
                cv[b, :, a * vc : (a + 1) * vc] = part[q] + contribution(q, 2)
            for e in range(NX * NC):
                for to in (up, down):
                    send(cv.at[b], ob.at[yh, me, b], fsend, frecv, device(e // 2, to, z, e % 2))
    with scope("f_recv"):
        wait_for(ob, frecv)
    wide = half // NB
    for h in range(2):
        for b in range(NB):
            whole = ob[h, 0, b]
            for e in range(1, NX * NC):
                whole += ob[h, e, b]
            at = h * half + b * wide
            out[:, at : at + wide] = whole * scale

    wait_for(det_v, ysend.at[0])
    wait_for(src_v, ysend.at[1])
    wait_for(pr_in, ysend.at[2])
    wait_for(S.at[:, own], xsend.at[0])
    for i in (1, 2, 3):
        wait_for(D.at[:, own], xsend.at[i])
    wait_for(tx.at[:, pl.ds(0, 3)], rsend)
    wait_for(zr.at[pl.ds(0, NZ - 1)], zsend)
    wait_for(zr.at[pl.ds(0, NZ - 1)], gsend)
    wait_for(M.at[:, pl.ds(0, 3)], asend)
    wait_for(ob, fsend)


def shards(src_fields, det_fields, probes):
    rows, voxels = src_fields.shape
    half = voxels // 2
    vc = half // NQ
    sources, detectors = rows * lax.axis_size("blk"), det_fields.shape[0] * lax.axis_size("blk")
    scale = 1.0 / (sources * detectors)
    any_spec = pl.BlockSpec(memory_space=pl.ANY)
    return pl.pallas_call(
        functools.partial(kernel, scale),
        out_shape=jax.ShapeDtypeStruct((2, voxels), F32),
        in_specs=[any_spec] * 3,
        out_specs=pl.BlockSpec(memory_space=pltpu.VMEM),
        scratch_shapes=[
            pltpu.VMEM((64, voxels), BF16),
            pltpu.VMEM((64, voxels), BF16),
            pltpu.VMEM((2, voxels), BF16),
            pltpu.VMEM((2, half), BF16),
            pltpu.VMEM((NQ, 256, vc), BF16),
            pltpu.VMEM((NQ, 512, vc), BF16),
            pltpu.VMEM((4, 4, 2, 64, 128), F32),
            pltpu.VMEM((4, 4, 2, 64, 128), BF16),
            pltpu.VMEM((4, 4, 2, 64, 128), BF16),
            pltpu.VMEM((4, 4, 2, 16, 128), BF16),
            pltpu.VMEM((NZ, 2, 16, 128), BF16),
            pltpu.VMEM((2, 16, 128), BF16),
            pltpu.VMEM((4, 4, 4, 2, 16, 128), BF16),
            pltpu.VMEM((NQ, 2, vc), F32),
            pltpu.VMEM((NB, 2, half // NB), F32),
            pltpu.VMEM((2, NX * NC, NB, 2, half // NB), F32),
            DMA((NQ + 1,)),
            DMA((3,)),
            DMA((NQ,)),
            DMA((NQ,)),
            DMA,
            DMA((4,)),
            DMA((NQ,)),
            DMA((NQ,)),
            DMA((NQ,)),
            DMA((NQ,)),
            DMA,
            DMA((4,)),
            DMA,
            DMA,
            DMA,
            DMA((4,)),
            DMA,
            DMA((4,)),
            DMA,
            DMA,
            pltpu.SemaphoreType.REGULAR((3,)),
        ],
        compiler_params=pltpu.CompilerParams(collective_id=0, has_side_effects=True),
        name="gauss_newton",
    )(src_fields, det_fields, probes)


def solution(mesh):
    return jax.shard_map(
        shards,
        mesh=mesh,
        in_specs=(P("blk", "vox"), P("blk", "vox"), P(None, "vox")),
        out_specs=P(None, "vox"),
        check_vma=False,
    )
```

time: 212 us -> 70 us (0.33)
  waiting for transfers between devices: 113 us -> 0 us
  Pallas kernels: 0 us -> 68.3 us
  blocking collectives: 62.5 us -> 0 us
  between operations: 13.5 us -> 0.01 us
  matrix products: 11.3 us -> 0 us
  local copies, waits for them, and re-layouts: 5.94 us -> 1.38 us
  starting transfers between devices: 4.23 us -> 0 us
    all_gather x1 -> x0, waiting for transfers between devices: 92.7 us -> none  [shards(): portion = lax.all_gather(det_fields, 'blk', axis=0, tiled=True)]
    pallas_call x0 -> x1, Pallas kernels: none -> 68.3 us  [shards(): pl.pallas_call(functools.partial(kernel, scale), out_shape=jax.ShapeDtype...]
    all_to_all x2 -> x0, blocking collectives: 62.5 us -> none  [the longest x1 44.3 us: summed_on_arrival(): tiles = lax.all_to_all(cut_along(value, dim, count), axis, 0, 0, tiled=True)]
    all_to_all x1 -> x0, waiting for transfers between devices: 19.7 us -> none  [from_everyone(): return lax.all_to_all(copies, axis, split_axis=0, concat_axis=0, tiled=True)]
    dot_general x2 -> x0, matrix products: 11.3 us -> none  [the longest x1 6.6 us: shards(): jnp.einsum('rv,dv->rd', weighted, portion, preferred_element_type=jnp.flo...]
    mul x3 -> x0, local copies, waits for them, and re-layouts: 4.55 us -> none  [the longest x2 4.52 us: shards(): contrib = jnp.sum(src_fields.astype(jnp.float32)[None] * backproj, axis=1)]
    all_to_all x1 -> x0, starting transfers between devices: 4.23 us -> none  [from_everyone(): return lax.all_to_all(copies, axis, split_axis=0, concat_axis=0, tiled=True)]
  transfers between devices with their start and end apart: 2 -> 0, of which waited for: 2 -> 0; matrix products, arithmetic and copies ran while one was open for 2% -> 0% of each run, Pallas kernels for 0% -> 0%
where the time goes in v2:
time: 70 us; the launch traced here: 69.7 us
  Pallas kernels  68.3 us (98%)
  local copies, waits for them, and re-layouts  1.38 us (2%)
    pallas_call x1, Pallas kernels, shards(): pl.pallas_call(functools.partial(kernel, scale), out_shape=jax.ShapeDtype...  68.3 us

profile of v2, /device:TPU:1, one launch (start us, length us, event | category | flops | bytes accessed | tf_op | source)
XLA Modules:
  0.0 69.7 jit_solution(3208663812647710539)
XLA Ops:
  0.0 68.3 %gauss_newton.1 = f32[2,4096]{1,0:T(2,128)} custom-call(bf16[64,4096]{1,0:T(8,128)(2,1)} %src_hbm.1, bf16[64,4096]{1,0:T(8,128)(2,1)} %det_hbm.1, bf16[2,4096]{1,0:T(2,128)(2,1)} %probes_hbm.1), custom_call_target="tpu_custom_call" | custom-call | tf_op jit(solution)/shard_map/gauss_newton/pallas_call | solution.py:295
  68.3 1.4 %copy.5 = f32[2,4096]{1,0:T(2,128)} copy(f32[2,4096]{1,0:T(2,128)} %gauss_newton.1) | data formatting | bytes 65536

commit v3 on v2

v3 whole, which is shorter than its diff:
```python
import functools

import jax
import jax.numpy as jnp
from jax import lax
from jax.experimental import pallas as pl
from jax.experimental.pallas import tpu as pltpu
from jax.sharding import PartitionSpec as P

MESH = pl.DeviceIdType.MESH
BF16 = jnp.bfloat16
F32 = jnp.float32
DMA = pltpu.SemaphoreType.DMA

NX, NY, NZ, NC = 4, 4, 16, 2
NQ = 8
NB = 4


def device(x, y, z, c):
    return (x * 4 + (y // 2) * 2 + c, z * 2 + y % 2)


def send(src, dst, send_sem, recv_sem, to):
    pltpu.make_async_remote_copy(
        src_ref=src, dst_ref=dst, send_sem=send_sem, recv_sem=recv_sem, device_id=to, device_id_type=MESH
    ).start()


def wait_for(ref, sem):
    pltpu.make_async_copy(ref, ref, sem).wait()


def kernel(
    scale,
    src_hbm,
    det_hbm,
    probes_hbm,
    out,
    src_v,
    det_v,
    pr_v,
    pr_in,
    S,
    D,
    acc,
    tx,
    rx,
    zs,
    zr,
    mz,
    M,
    part,
    cv,
    ob,
    ld,
    ysend,
    yS,
    yD,
    pS,
    xsend,
    xS,
    xD,
    c0,
    c1,
    rsend,
    rrecv,
    zsend,
    zrecv,
    gsend,
    grecv,
    asend,
    arecv,
    fsend,
    frecv,
    ready,
):
    blk = lax.axis_index("blk")
    vox = lax.axis_index("vox")
    x, yh, c = blk // 4, (blk // 2) % 2, blk % 2
    z, yl = vox // 2, vox % 2
    y = yh * 2 + yl
    half = src_v.shape[1] // 2
    vc = half // NQ
    scope = jax.named_scope

    up, down = (y + 1) % NY, (y + 3) % NY
    xs = (x // 2) * 2 + 1 - x % 2
    xd = 3 - x
    me = x * 2 + c
    dev_up, dev_down = device(x, up, z, c), device(x, down, z, c)
    dev_xs, dev_xd = device(xs, y, z, c), device(xd, y, z, c)
    dev_c = device(x, y, z, 1 - c)

    def dev_z(d):
        return device(x, y, (z + NZ + d) % NZ, c)

    def signal(sem, to):
        pl.semaphore_signal(sem, inc=1, device_id=to, device_id_type=MESH)

    barrier = pltpu.get_barrier_semaphore()
    near = (dev_up, dev_down, dev_xs, dev_xd, dev_c, dev_z(1), dev_z(-1))
    for to in near:
        signal(barrier, to)

    h_up, h_down = up // 2, down // 2

    parts = [(q, 0, vc) for q in range(NQ - 1)] + [(NQ - 1, 0, vc // 2), (NQ - 1, vc // 2, vc // 2)]

    def columns(h, q, lo, wide):
        return pl.ds(pl.multiple_of(h * half + q * vc + lo, wide), wide)

    pltpu.make_async_copy(probes_hbm, pr_v, ld.at[NQ]).start()
    for q in range(0, NQ, 2):
        for h in range(2):
            at = pl.ds(h * half + q * vc, 2 * vc)
            pltpu.make_async_copy(det_hbm.at[:, at], det_v.at[:, at], ld.at[q]).start()
            pltpu.make_async_copy(src_hbm.at[:, at], src_v.at[:, at], ld.at[q]).start()
    with scope("t_barrier"):
        pl.semaphore_wait(barrier, len(near))

    def spread_word(r):
        d = 2**r
        if r:
            pl.semaphore_wait(ready.at[r - 1], 2)
        if r < 3:
            signal(ready.at[r], dev_z(d))
            signal(ready.at[r], dev_z(-d))

    mine = pl.ds(pl.multiple_of(yh * 64, 64), 64)
    own, other = pl.ds(0, 128), pl.ds(128, 128)
    for n, (q, lo, wide) in enumerate(parts):
        if q % 2 == 0:
            wait_for(D.at[q], ld.at[q])
        to = (q, mine, pl.ds(lo, wide))
        for fields, here, i, sem in ((det_v, D, 0, yD), (src_v, S, 1, yS)):
            send(fields.at[:, columns(h_up, q, lo, wide)], here.at[to], ysend.at[i], sem.at[n], dev_up)
            send(fields.at[:, columns(h_down, q, lo, wide)], here.at[to], ysend.at[i], sem.at[n], dev_down)
        if n == 0:
            wait_for(pr_v, ld.at[NQ])
            send(
                pr_v.at[:, pl.ds(pl.multiple_of(h_up * half, half), half)],
                pr_in,
                ysend.at[2],
                pS,
                dev_up,
            )
            spread_word(0)

    def pass_own(n):
        q, at = parts[n][0], pl.ds(*parts[n][1:])
        wait_for(D.at[q, own, at], yD.at[n])
        send(D.at[q, own, at], D.at[q, other, at], xsend.at[1], xD.at[n], dev_xd)
        send(D.at[q, own, at], D.at[q, pl.ds(256, 128), at], xsend.at[2], c0.at[n], dev_c)
        wait_for(S.at[q, own, at], yS.at[n])
        send(S.at[q, own, at], S.at[q, other, at], xsend.at[0], xS.at[n], dev_xs)

    def pass_other(n):
        q, at = parts[n][0], pl.ds(*parts[n][1:])
        wait_for(D.at[q, other, at], xD.at[n])
        send(D.at[q, other, at], D.at[q, pl.ds(384, 128), at], xsend.at[3], c1.at[n], dev_c)

    def measure(q):
        for n, (of, lo, wide) in enumerate(parts):
            if of == q:
                at = pl.ds(lo, wide)
                wait_for(S.at[q, other, at], xS.at[n])
                wait_for(D.at[q, pl.ds(256, 128), at], c0.at[n])
                wait_for(D.at[q, pl.ds(384, 128), at], c1.at[n])
        fields = S[q].astype(F32)
        p = pr_in[:, q * vc : (q + 1) * vc].astype(F32)
        det = D[q]
        for k in range(2):
            weighted = (fields * p[k : k + 1]).astype(BF16)
            sums = lax.dot_general(weighted, det, (((1,), (1,)), ((), ())), preferred_element_type=F32)
            for g in range(4):
                piece = sums[:, g * 128 : (g + 1) * 128].reshape(4, 2, 32, 128)
                for h in range(2):
                    if q:
                        acc[2 * g + h, :, k] += piece[:, h]
                    else:
                        acc[2 * g + h, :, k] = piece[:, h]

    word = {1: 1, 4: 2}
    for t in range(len(parts) + 4):
        if t < len(parts):
            with scope("g%02d_own" % t):
                pass_own(t)
        if t in word:
            with scope("g%02d_word" % t):
                spread_word(word[t])
        if 0 <= t - 3 < len(parts):
            with scope("g%02d_other" % t):
                pass_other(t - 3)
        if t == 4:
            wait_for(pr_in, pS)
        if 0 <= t - 4 < NQ - 1:
            with scope("g%02d_meas" % t):
                measure(t - 4)
    with scope("g99_meas"):
        measure(NQ - 1)

    pairs = NZ // 2
    zp, zb = z // 2, z % 2
    s = 1 - 2 * zb
    away = (4, 3 * s, -3 * s, 2 * s, -2 * s, s, -s, 0)
    groups = [(zp + pairs + o) % pairs for o in away]
    for i, g in enumerate(groups):
        for d in (2, 1, 3):
            to = (y + d) % NY
            tx[i, to] = acc[g, to].astype(BF16)
            send(tx.at[i, to], rx.at[i, y], rsend, rrecv.at[i], device(x, to, z, c))
    spread_word(3)

    for i, g in enumerate(groups):
        with scope("r%d_y" % i):
            wait_for(rx.at[i, pl.ds(0, 3)], rrecv.at[i])
        total = acc[g, y]
        for d in (1, 2, 3):
            total += rx[i, (y + d) % NY].astype(F32)
        total = total.astype(BF16)
        for k in range(2):
            zs[i, :, k] = total[k].reshape(2, 16, 128)
        if i < pairs - 1:
            for b in (0, 1):
                send(zs.at[i, b], zr.at[z], zsend, zrecv, device(x, y, g * 2 + b, c))
        else:
            send(zs.at[i, 1 - zb], zr.at[z], zsend, zrecv, device(x, y, g * 2 + 1 - zb, c))
    zr[z] = zs[pairs - 1, zb]
    with scope("r_z"):
        wait_for(zr.at[pl.ds(0, NZ - 1)], zrecv)
    total = zr[0].astype(F32)
    for j in range(1, NZ):
        total += zr[j].astype(F32)
    mz[...] = total.astype(BF16)

    M[zp, y, zb] = mz[...]
    for step in range(1, NZ // 2 + 1):
        for to in (step, -step)[: 1 if step == NZ // 2 else 2]:
            send(mz, M.at[zp, y, zb], gsend, grecv.at[zp], dev_z(to))

    back = groups[::-1]
    for i, g in enumerate(back):
        with scope("b%d_z" % i):
            wait_for(zr.at[pl.ds(0, 2 if i else 1)], grecv.at[g])
        for d in (2, 1, 3):
            send(M.at[g, y], M.at[g, y], asend, arecv.at[g], device(x, (y + d) % NY, z, c))

    block, side = zp // 2, 2 * (zp % 2) - 1
    blocks = [(block + o) % 4 for o in (0, 4 + side, 4 - side, 2)]

    def arrived(g):
        for h in range(2):
            wait_for(M.at[2 * g + h, pl.ds(0, 3)], arecv.at[2 * g + h])

    def contribution(q, lo):
        two = blocks[lo : lo + 2]
        lhs = jnp.concatenate([M[pl.ds(2 * g, 2)].reshape(512, 128) for g in two], axis=1)
        det = jnp.concatenate([D[q, pl.ds(pl.multiple_of(g * 128, 128), 128)] for g in two], axis=0)
        bp = jnp.dot(lhs, det, preferred_element_type=F32).reshape(2, 4, 2, 2, 16, vc)
        fields = S[q].astype(F32).reshape(4, 2, 2, 16, vc)
        sums = []
        for k in range(2):
            row = jnp.zeros((8, vc), F32)
            for h in range(2):
                for b in range(2):
                    row += jnp.sum((fields[:, h, b] * bp[h, :, b, k]).reshape(8, 8, vc), axis=0)
            sums.append(row)
        return sums

    arrived(blocks[0])
    with scope("b1_y"):
        arrived(blocks[1])
    with scope("m_front"):
        for q in range(NQ):
            part[q, 0], part[q, 1] = contribution(q, 0)
    with scope("b2_y"):
        arrived(blocks[2])
    with scope("b3_y"):
        arrived(blocks[3])

    per = NQ // NB
    with scope("m_rest"):
        for n in range(NB):
            rows = [[], []]
            for q in range(n * per, (n + 1) * per):
                for k, sums in enumerate(contribution(q, 2)):
                    row = jnp.sum(part[q, k] + sums, axis=0, keepdims=True)
                    rows[k] += [row[:, i * 128 : (i + 1) * 128] for i in range(vc // 128)]
            cv[n] = jnp.concatenate(rows[0] + rows[1], axis=0).reshape(-1, 8, 128)
            for e in range(NX * NC):
                for to in (up, down):
                    send(cv.at[n], ob.at[yh, me, n], fsend, frecv, device(e // 2, to, z, e % 2))
    with scope("f_recv"):
        wait_for(ob, frecv)
    wide = half // NB
    for h in range(2):
        for n in range(NB):
            whole = ob[h, 0, n]
            for e in range(1, NX * NC):
                whole += ob[h, e, n]
            whole = (whole * scale).reshape(-1, 128)
            for k in range(2):
                for i in range(wide // 128):
                    at = h * half + n * wide + i * 128
                    row = k * (wide // 128) + i
                    out[k : k + 1, at : at + 128] = whole[row : row + 1]

    wait_for(det_v, ysend.at[0])
    wait_for(src_v, ysend.at[1])
    wait_for(pr_in, ysend.at[2])
    wait_for(S.at[:, own], xsend.at[0])
    for i in (1, 2, 3):
        wait_for(D.at[:, own], xsend.at[i])
    wait_for(tx.at[:, pl.ds(0, 3)], rsend)
    wait_for(zr.at[pl.ds(0, NZ - 1)], zsend)
    wait_for(zr.at[pl.ds(0, NZ - 1)], gsend)
    wait_for(M.at[:, pl.ds(0, 3)], asend)
    wait_for(ob, fsend)


def shards(src_fields, det_fields, probes):
    rows, voxels = src_fields.shape
    half = voxels // 2
    vc = half // NQ
    sources, detectors = rows * lax.axis_size("blk"), det_fields.shape[0] * lax.axis_size("blk")
    scale = 1.0 / (sources * detectors)
    hbm = pl.BlockSpec(memory_space=pl.ANY)
    return pl.pallas_call(
        functools.partial(kernel, scale),
        out_shape=jax.ShapeDtypeStruct((2, voxels), F32),
        in_specs=[hbm] * 3,
        out_specs=pl.BlockSpec(memory_space=pltpu.VMEM),
        scratch_shapes=[
            pltpu.VMEM((64, voxels), BF16),
            pltpu.VMEM((64, voxels), BF16),
            pltpu.VMEM((2, voxels), BF16),
            pltpu.VMEM((2, half), BF16),
            pltpu.VMEM((NQ, 256, vc), BF16),
            pltpu.VMEM((NQ, 512, vc), BF16),
            pltpu.VMEM((8, 4, 2, 32, 128), F32),
            pltpu.VMEM((8, 4, 2, 32, 128), BF16),
            pltpu.VMEM((8, 4, 2, 32, 128), BF16),
            pltpu.VMEM((8, 2, 2, 16, 128), BF16),
            pltpu.VMEM((NZ, 2, 16, 128), BF16),
            pltpu.VMEM((2, 16, 128), BF16),
            pltpu.VMEM((8, 4, 2, 2, 16, 128), BF16),
            pltpu.VMEM((NQ, 2, 8, vc), F32),
            pltpu.VMEM((NB, half // NB // 512, 8, 128), F32),
            pltpu.VMEM((2, NX * NC, NB, half // NB // 512, 8, 128), F32),
            DMA((NQ + 1,)),
            DMA((3,)),
            DMA((NQ + 1,)),
            DMA((NQ + 1,)),
            DMA,
            DMA((4,)),
            DMA((NQ + 1,)),
            DMA((NQ + 1,)),
            DMA((NQ + 1,)),
            DMA((NQ + 1,)),
            DMA,
            DMA((8,)),
            DMA,
            DMA,
            DMA,
            DMA((8,)),
            DMA,
            DMA((8,)),
            DMA,
            DMA,
            pltpu.SemaphoreType.REGULAR((3,)),
        ],
        compiler_params=pltpu.CompilerParams(
            collective_id=0, has_side_effects=True, vmem_limit_bytes=60 * 2**20
        ),
        name="gauss_newton",
    )(src_fields, det_fields, probes)


def solution(mesh):
    return jax.shard_map(
        shards,
        mesh=mesh,
        in_specs=(P("blk", "vox"), P("blk", "vox"), P(None, "vox")),
        out_specs=P(None, "vox"),
        check_vma=False,
    )
```

time: 70 us -> 69.2 us (0.989)
  Pallas kernels: 68.3 us -> 67.6 us
where the time goes in v3:
time: 69.2 us; the launch traced here: 69 us
  Pallas kernels  67.6 us (98%)
  local copies, waits for them, and re-layouts  1.38 us (2%)
    pallas_call x1, Pallas kernels, shards(): pl.pallas_call(functools.partial(kernel, scale), out_shape=jax.ShapeDtype...  67.6 us

profile of v3, /device:TPU:1, one launch (start us, length us, event | category | flops | bytes accessed | tf_op | source)
XLA Modules:
  0.0 69.0 jit_solution(5957855920995926126)
XLA Ops:
  0.0 67.6 %gauss_newton.1 = f32[2,4096]{1,0:T(2,128)} custom-call(bf16[64,4096]{1,0:T(8,128)(2,1)} %src_hbm.1, bf16[64,4096]{1,0:T(8,128)(2,1)} %det_hbm.1, bf16[2,4096]{1,0:T(2,128)(2,1)} %probes_hbm.1), custom_call_target="tpu_custom_call" | custom-call | tf_op jit(solution)/shard_map/gauss_newton/pallas_call | solution.py:329
  67.6 1.4 %copy.5 = f32[2,4096]{1,0:T(2,128)} copy(f32[2,4096]{1,0:T(2,128)} %gauss_newton.1) | data formatting | bytes 65536

commit v4 on v3

v4 whole, which is shorter than its diff:
```python
import functools

import jax
import jax.numpy as jnp
from jax import lax
from jax.experimental import pallas as pl
from jax.experimental.pallas import tpu as pltpu
from jax.sharding import PartitionSpec as P

MESH = pl.DeviceIdType.MESH
BF16 = jnp.bfloat16
F32 = jnp.float32
DMA = pltpu.SemaphoreType.DMA

NX, NY, NZ, NC = 4, 4, 16, 2
NQ = 8
NB = 2


def device(x, y, z, c):
    return (x * 4 + (y // 2) * 2 + c, z * 2 + y % 2)


def send(src, dst, send_sem, recv_sem, to):
    pltpu.make_async_remote_copy(
        src_ref=src, dst_ref=dst, send_sem=send_sem, recv_sem=recv_sem, device_id=to, device_id_type=MESH
    ).start()


def wait_for(ref, sem):
    pltpu.make_async_copy(ref, ref, sem).wait()


def kernel(
    scale,
    src_hbm,
    det_hbm,
    probes_hbm,
    out,
    src_v,
    det_v,
    pr_v,
    pr_in,
    S,
    D,
    acc,
    tx,
    rx,
    zs,
    zr,
    mz,
    M,
    part,
    cv,
    ob,
    ld,
    ysend,
    yS,
    yD,
    pS,
    xsend,
    xS,
    xD,
    c0,
    c1,
    rsend,
    rrecv,
    zsend,
    zrecv,
    gsend,
    grecv,
    asend,
    arecv,
    fsend,
    frecv,
    ready,
):
    blk = lax.axis_index("blk")
    vox = lax.axis_index("vox")
    x, yh, c = blk // 4, (blk // 2) % 2, blk % 2
    z, yl = vox // 2, vox % 2
    y = yh * 2 + yl
    half = src_v.shape[1] // 2
    vc = half // NQ
    scope = jax.named_scope

    up, down = (y + 1) % NY, (y + 3) % NY
    xs = (x // 2) * 2 + 1 - x % 2
    xd = 3 - x
    me = x * 2 + c
    dev_up, dev_down = device(x, up, z, c), device(x, down, z, c)
    dev_xs, dev_xd = device(xs, y, z, c), device(xd, y, z, c)
    dev_c = device(x, y, z, 1 - c)

    def dev_z(d):
        return device(x, y, (z + NZ + d) % NZ, c)

    def signal(sem, to):
        pl.semaphore_signal(sem, inc=1, device_id=to, device_id_type=MESH)

    barrier = pltpu.get_barrier_semaphore()
    near = (dev_up, dev_down, dev_xs, dev_xd, dev_c, dev_z(1), dev_z(-1))
    for to in near:
        signal(barrier, to)

    h_up, h_down = up // 2, down // 2

    parts = [(q, 0, vc) for q in range(NQ - 1)] + [(NQ - 1, 0, vc // 2), (NQ - 1, vc // 2, vc // 2)]

    def columns(h, q, lo, wide):
        return pl.ds(pl.multiple_of(h * half + q * vc + lo, wide), wide)

    pltpu.make_async_copy(probes_hbm, pr_v, ld.at[NQ]).start()
    for q in range(0, NQ, 2):
        for h in range(2):
            at = pl.ds(h * half + q * vc, 2 * vc)
            pltpu.make_async_copy(det_hbm.at[:, at], det_v.at[:, at], ld.at[q]).start()
            pltpu.make_async_copy(src_hbm.at[:, at], src_v.at[:, at], ld.at[q + 1]).start()
    with scope("t_barrier"):
        pl.semaphore_wait(barrier, len(near))

    def spread_word(r):
        d = 2**r
        if r:
            pl.semaphore_wait(ready.at[r - 1], 2)
        if r < 3:
            signal(ready.at[r], dev_z(d))
            signal(ready.at[r], dev_z(-d))

    mine = pl.ds(pl.multiple_of(yh * 64, 64), 64)
    own, other = pl.ds(0, 128), pl.ds(128, 128)
    LEAD = 2
    last = len(parts)

    def swap(fields, here, i, sem, n):
        q, lo, wide = parts[n]
        if q % 2 == 0:
            wait_for(D.at[q, pl.ds(0, 256)], ld.at[q + i])
        to = (q, mine, pl.ds(lo, wide))
        send(fields.at[:, columns(h_up, q, lo, wide)], here.at[to], ysend.at[i], sem.at[n], dev_up)
        send(fields.at[:, columns(h_down, q, lo, wide)], here.at[to], ysend.at[i], sem.at[n], dev_down)

    for t in range(last + LEAD):
        if t < last:
            swap(det_v, D, 0, yD, t)
        if t >= LEAD:
            swap(src_v, S, 1, yS, t - LEAD)
        if t == 0:
            wait_for(pr_v, ld.at[NQ])
            send(
                pr_v.at[:, pl.ds(pl.multiple_of(h_up * half, half), half)],
                pr_in,
                ysend.at[2],
                pS,
                dev_up,
            )
            spread_word(0)

    def pass_det(n):
        q, at = parts[n][0], pl.ds(*parts[n][1:])
        wait_for(D.at[q, own, at], yD.at[n])
        send(D.at[q, own, at], D.at[q, other, at], xsend.at[1], xD.at[n], dev_xd)
        send(D.at[q, own, at], D.at[q, pl.ds(256, 128), at], xsend.at[2], c0.at[n], dev_c)

    def pass_src(n):
        q, at = parts[n][0], pl.ds(*parts[n][1:])
        wait_for(S.at[q, own, at], yS.at[n])
        send(S.at[q, own, at], S.at[q, other, at], xsend.at[0], xS.at[n], dev_xs)

    def pass_other(n):
        q, at = parts[n][0], pl.ds(*parts[n][1:])
        wait_for(D.at[q, other, at], xD.at[n])
        send(D.at[q, other, at], D.at[q, pl.ds(384, 128), at], xsend.at[3], c1.at[n], dev_c)

    def measure(n):
        q, lo, wide = parts[n]
        at = pl.ds(lo, wide)
        wait_for(D.at[q, pl.ds(256, 128), at], c0.at[n])
        wait_for(D.at[q, pl.ds(384, 128), at], c1.at[n])
        wait_for(S.at[q, other, at], xS.at[n])
        fields = S[q, :, at].astype(F32)
        p = pr_in[:, q * vc + lo : q * vc + lo + wide].astype(F32)
        det = D[q, :, at]
        for k in range(2):
            weighted = (fields * p[k : k + 1]).astype(BF16)
            sums = lax.dot_general(weighted, det, (((1,), (1,)), ((), ())), preferred_element_type=F32)
            for g in range(4):
                piece = sums[:, g * 128 : (g + 1) * 128].reshape(4, 2, 32, 128)
                for h in range(2):
                    if n:
                        acc[k, 2 * g + h] += piece[:, h]
                    else:
                        acc[k, 2 * g + h] = piece[:, h]

    word = {1: 1, 4: 2}
    for t in range(last + 5):
        if t < last:
            with scope("g%02d_det" % t):
                pass_det(t)
        if 0 <= t - LEAD < last:
            with scope("g%02d_src" % t):
                pass_src(t - LEAD)
        if t in word:
            with scope("g%02d_word" % t):
                spread_word(word[t])
        if 0 <= t - 3 < last:
            with scope("g%02d_other" % t):
                pass_other(t - 3)
        if t == 5:
            wait_for(pr_in, pS)
        if 0 <= t - 5 < last:
            with scope("g%02d_meas" % t):
                measure(t - 5)

    pairs = NZ // 2
    zp, zb = z // 2, z % 2
    s = 1 - 2 * zb
    away = (4, 3 * s, -3 * s, 2 * s, -2 * s, s, -s, 0)
    groups = [(zp + pairs + o) % pairs for o in away]
    for k in range(2):
        for i, g in enumerate(groups):
            for d in (2, 1, 3):
                to = (y + d) % NY
                tx[k, i, to] = acc[k, g, to].astype(BF16)
                send(tx.at[k, i, to], rx.at[k, i, y], rsend, rrecv.at[k, i], device(x, to, z, c))
    spread_word(3)

    def along_z(k):
        for i, g in enumerate(groups):
            with scope("r%d%d_y" % (k, i)):
                wait_for(rx.at[k, i, pl.ds(0, 3)], rrecv.at[k, i])
            total = acc[k, g, y]
            for d in (1, 2, 3):
                total += rx[k, i, (y + d) % NY].astype(F32)
            zs[k, i] = total.astype(BF16).reshape(2, 16, 128)
            for b in (0, 1) if i < pairs - 1 else (1 - zb,):
                send(zs.at[k, i, b], zr.at[k, z], zsend, zrecv.at[k], device(x, y, g * 2 + b, c))
        zr[k, z] = zs[k, pairs - 1, zb]

    def back_along_z(k):
        with scope("r%d_z" % k):
            wait_for(zr.at[k, pl.ds(0, NZ - 1)], zrecv.at[k])
        total = zr[k, 0].astype(F32)
        for j in range(1, NZ):
            total += zr[k, j].astype(F32)
        mz[k] = total.astype(BF16)
        M[k, zp, y, zb] = mz[k]
        for step in range(NZ // 2, 0, -1):
            for to in (step, -step)[: 1 if step == NZ // 2 else 2]:
                send(mz.at[k], M.at[k, zp, y, zb], gsend, grecv.at[k, zp], dev_z(to))

    back = groups[::-1]

    def back_along_y(k):
        for i, g in enumerate(back):
            with scope("b%d%d_z" % (k, i)):
                wait_for(zr.at[k, pl.ds(0, 2 if i else 1)], grecv.at[k, g])
            for d in (2, 1, 3):
                send(M.at[k, g, y], M.at[k, g, y], asend, arecv.at[k, g], device(x, (y + d) % NY, z, c))

    block, side = zp // 2, 2 * (zp % 2) - 1
    blocks = [(block + o) % 4 for o in (0, 4 + side, 4 - side, 2)]

    def arrived(k, g):
        for h in range(2):
            wait_for(M.at[k, 2 * g + h, pl.ds(0, 3)], arecv.at[k, 2 * g + h])

    def contribution(k, q, lo):
        two = blocks[lo : lo + 2]
        lhs = jnp.concatenate([M[k, pl.ds(2 * g, 2)].reshape(256, 128) for g in two], axis=1)
        det = jnp.concatenate([D[q, pl.ds(pl.multiple_of(g * 128, 128), 128)] for g in two], axis=0)
        bp = jnp.dot(lhs, det, preferred_element_type=F32).reshape(2, 4, 32, vc)
        fields = S[q].astype(F32).reshape(4, 2, 32, vc)
        row = jnp.zeros((8, vc), F32)
        for h in range(2):
            row += jnp.sum((fields[:, h] * bp[h]).reshape(16, 8, vc), axis=0)
        return row

    def front(k):
        with scope("m%d_front" % k):
            arrived(k, blocks[0])
            arrived(k, blocks[1])
            for q in range(NQ):
                part[k, q] = contribution(k, q, 0)

    def rest(k):
        with scope("m%d_y" % k):
            arrived(k, blocks[2])
            arrived(k, blocks[3])
        per = NQ // NB
        with scope("m%d_rest" % k):
            for n in range(NB):
                rows = []
                for q in range(n * per, (n + 1) * per):
                    row = jnp.sum(part[k, q] + contribution(k, q, 2), axis=0, keepdims=True)
                    rows += [row[:, i * 128 : (i + 1) * 128] for i in range(vc // 128)]
                cv[k, n] = jnp.concatenate(rows, axis=0)
                for e in range(NX * NC):
                    for to in (up, down):
                        send(cv.at[k, n], ob.at[k, yh, me, n], fsend, frecv.at[k], device(e // 2, to, z, e % 2))

    def finish(k):
        with scope("f%d_recv" % k):
            wait_for(ob.at[k], frecv.at[k])
        wide = half // NB
        for h in range(2):
            for n in range(NB):
                whole = ob[k, h, 0, n]
                for e in range(1, NX * NC):
                    whole += ob[k, h, e, n]
                whole = whole * scale
                for i in range(wide // 128):
                    at = h * half + n * wide + i * 128
                    out[k : k + 1, at : at + 128] = whole[i : i + 1]

    along_z(0)
    along_z(1)
    back_along_z(0)
    back_along_z(1)
    back_along_y(0)
    back_along_y(1)
    front(0)
    rest(0)
    front(1)
    rest(1)
    finish(0)
    finish(1)

    wait_for(det_v, ysend.at[0])
    wait_for(src_v, ysend.at[1])
    wait_for(pr_in, ysend.at[2])
    wait_for(S.at[:, own], xsend.at[0])
    for i in (1, 2, 3):
        wait_for(D.at[:, own], xsend.at[i])
    wait_for(tx.at[:, :, pl.ds(0, 3)], rsend)
    wait_for(zr.at[:, pl.ds(0, NZ - 1)], zsend)
    wait_for(zr.at[:, pl.ds(0, NZ - 1)], gsend)
    wait_for(M.at[:, :, pl.ds(0, 3)], asend)
    wait_for(ob, fsend)


def shards(src_fields, det_fields, probes):
    rows, voxels = src_fields.shape
    half = voxels // 2
    vc = half // NQ
    sources, detectors = rows * lax.axis_size("blk"), det_fields.shape[0] * lax.axis_size("blk")
    scale = 1.0 / (sources * detectors)
    hbm = pl.BlockSpec(memory_space=pl.ANY)
    return pl.pallas_call(
        functools.partial(kernel, scale),
        out_shape=jax.ShapeDtypeStruct((2, voxels), F32),
        in_specs=[hbm] * 3,
        out_specs=pl.BlockSpec(memory_space=pltpu.VMEM),
        scratch_shapes=[
            pltpu.VMEM((64, voxels), BF16),
            pltpu.VMEM((64, voxels), BF16),
            pltpu.VMEM((2, voxels), BF16),
            pltpu.VMEM((2, half), BF16),
            pltpu.VMEM((NQ, 256, vc), BF16),
            pltpu.VMEM((NQ, 512, vc), BF16),
            pltpu.VMEM((2, 8, 4, 32, 128), F32),
            pltpu.VMEM((2, 8, 4, 32, 128), BF16),
            pltpu.VMEM((2, 8, 4, 32, 128), BF16),
            pltpu.VMEM((2, 8, 2, 16, 128), BF16),
            pltpu.VMEM((2, NZ, 16, 128), BF16),
            pltpu.VMEM((2, 16, 128), BF16),
            pltpu.VMEM((2, 8, 4, 2, 16, 128), BF16),
            pltpu.VMEM((2, NQ, 8, vc), F32),
            pltpu.VMEM((2, NB, half // NB // 128, 128), F32),
            pltpu.VMEM((2, 2, NX * NC, NB, half // NB // 128, 128), F32),
            DMA((NQ + 1,)),
            DMA((3,)),
            DMA((NQ + 1,)),
            DMA((NQ + 1,)),
            DMA,
            DMA((4,)),
            DMA((NQ + 1,)),
            DMA((NQ + 1,)),
            DMA((NQ + 1,)),
            DMA((NQ + 1,)),
            DMA,
            DMA((2, 8)),
            DMA,
            DMA((2,)),
            DMA,
            DMA((2, 8)),
            DMA,
            DMA((2, 8)),
            DMA,
            DMA((2,)),
            pltpu.SemaphoreType.REGULAR((3,)),
        ],
        compiler_params=pltpu.CompilerParams(
            collective_id=0, has_side_effects=True, vmem_limit_bytes=60 * 2**20
        ),
        name="gauss_newton",
    )(src_fields, det_fields, probes)


def solution(mesh):
    return jax.shard_map(
        shards,
        mesh=mesh,
        in_specs=(P("blk", "vox"), P("blk", "vox"), P(None, "vox")),
        out_specs=P(None, "vox"),
        check_vma=False,
    )
```

time: 69.2 us -> 65.5 us (0.947)
  Pallas kernels: 67.6 us -> 63.9 us
    pallas_call x1, Pallas kernels: 67.6 us -> 63.9 us  [shards(): pl.pallas_call(functools.partial(kernel, scale), out_shape=jax.ShapeDtype...]
where the time goes in v4:
time: 65.5 us; the launch traced here: 65.3 us
  Pallas kernels  63.9 us (98%)
  local copies, waits for them, and re-layouts  1.38 us (2%)
    pallas_call x1, Pallas kernels, shards(): pl.pallas_call(functools.partial(kernel, scale), out_shape=jax.ShapeDtype...  63.9 us
    unnamed x1, local copies, waits for them, and re-layouts  1.38 us

profile of v4, /device:TPU:1, one launch (start us, length us, event | category | flops | bytes accessed | tf_op | source)
XLA Modules:
  0.0 65.3 jit_solution(16398528279872050325)
XLA Ops:
  0.0 63.9 %gauss_newton.1 = f32[2,4096]{1,0:T(2,128)} custom-call(bf16[64,4096]{1,0:T(8,128)(2,1)} %src_hbm.1, bf16[64,4096]{1,0:T(8,128)(2,1)} %det_hbm.1, bf16[2,4096]{1,0:T(2,128)(2,1)} %probes_hbm.1), custom_call_target="tpu_custom_call" | custom-call | tf_op jit(solution)/shard_map/gauss_newton/pallas_call | solution.py:349
  63.9 1.4 %copy.5 = f32[2,4096]{1,0:T(2,128)} copy(f32[2,4096]{1,0:T(2,128)} %gauss_newton.1) | data formatting | bytes 65536

commit v5 on v4

--- a/solution.py
+++ b/solution.py
@@ -105,7 +105,11 @@
 
     h_up, h_down = up // 2, down // 2
 
-    parts = [(q, 0, vc) for q in range(NQ - 1)] + [(NQ - 1, 0, vc // 2), (NQ - 1, vc // 2, vc // 2)]
+    parts = []
+    for q in range(NQ):
+        cuts = 2 if q in (0, NQ - 1) else 1
+        parts += [(q, i * vc // cuts, vc // cuts) for i in range(cuts)]
+    last = len(parts)
 
     def columns(h, q, lo, wide):
         return pl.ds(pl.multiple_of(h * half + q * vc + lo, wide), wide)
@@ -129,22 +133,17 @@
 
     mine = pl.ds(pl.multiple_of(yh * 64, 64), 64)
     own, other = pl.ds(0, 128), pl.ds(128, 128)
-    LEAD = 2
-    last = len(parts)
-
     def swap(fields, here, i, sem, n):
         q, lo, wide = parts[n]
-        if q % 2 == 0:
+        if q % 2 == 0 and lo == 0:
             wait_for(D.at[q, pl.ds(0, 256)], ld.at[q + i])
         to = (q, mine, pl.ds(lo, wide))
         send(fields.at[:, columns(h_up, q, lo, wide)], here.at[to], ysend.at[i], sem.at[n], dev_up)
         send(fields.at[:, columns(h_down, q, lo, wide)], here.at[to], ysend.at[i], sem.at[n], dev_down)
 
-    for t in range(last + LEAD):
-        if t < last:
-            swap(det_v, D, 0, yD, t)
-        if t >= LEAD:
-            swap(src_v, S, 1, yS, t - LEAD)
+    for t in range(last):
+        swap(det_v, D, 0, yD, t)
+        swap(src_v, S, 1, yS, t)
         if t == 0:
             wait_for(pr_v, ld.at[NQ])
             send(
@@ -156,21 +155,21 @@
             )
             spread_word(0)
 
-    def pass_det(n):
+    def pass_own(n):
         q, at = parts[n][0], pl.ds(*parts[n][1:])
         wait_for(D.at[q, own, at], yD.at[n])
         send(D.at[q, own, at], D.at[q, other, at], xsend.at[1], xD.at[n], dev_xd)
         send(D.at[q, own, at], D.at[q, pl.ds(256, 128), at], xsend.at[2], c0.at[n], dev_c)
-
-    def pass_src(n):
-        q, at = parts[n][0], pl.ds(*parts[n][1:])
+        if n == last - 1:
+            send(D.at[q, own, at], D.at[q, pl.ds(384, 128), at], xsend.at[3], c1.at[n], device(xd, y, z, 1 - c))
         wait_for(S.at[q, own, at], yS.at[n])
         send(S.at[q, own, at], S.at[q, other, at], xsend.at[0], xS.at[n], dev_xs)
 
     def pass_other(n):
         q, at = parts[n][0], pl.ds(*parts[n][1:])
         wait_for(D.at[q, other, at], xD.at[n])
-        send(D.at[q, other, at], D.at[q, pl.ds(384, 128), at], xsend.at[3], c1.at[n], dev_c)
+        if n < last - 1:
+            send(D.at[q, other, at], D.at[q, pl.ds(384, 128), at], xsend.at[3], c1.at[n], dev_c)
 
     def measure(n):
         q, lo, wide = parts[n]
@@ -192,49 +191,48 @@
                     else:
                         acc[k, 2 * g + h] = piece[:, h]
 
-    word = {1: 1, 4: 2}
-    for t in range(last + 5):
+    word = {3: 1, 6: 2}
+    for t in range(last + 6):
         if t < last:
-            with scope("g%02d_det" % t):
-                pass_det(t)
-        if 0 <= t - LEAD < last:
-            with scope("g%02d_src" % t):
-                pass_src(t - LEAD)
+            with scope("g%02d_own" % t):
+                pass_own(t)
         if t in word:
             with scope("g%02d_word" % t):
                 spread_word(word[t])
-        if 0 <= t - 3 < last:
+        if 0 <= t - 4 < last:
             with scope("g%02d_other" % t):
-                pass_other(t - 3)
-        if t == 5:
+                pass_other(t - 4)
+        if t == 6:
             wait_for(pr_in, pS)
-        if 0 <= t - 5 < last:
+        if 0 <= t - 6 < last:
             with scope("g%02d_meas" % t):
-                measure(t - 5)
+                measure(t - 6)
 
     pairs = NZ // 2
     zp, zb = z // 2, z % 2
     s = 1 - 2 * zb
     away = (4, 3 * s, -3 * s, 2 * s, -2 * s, s, -s, 0)
     groups = [(zp + pairs + o) % pairs for o in away]
+    turns = [(0, 0), (0, 1), (0, 2), (1, 0), (1, 1), (1, 2), (0, 3), (0, 4), (1, 3), (1, 4)]
+    turns += [(0, 5), (0, 6), (0, 7), (1, 5), (1, 6), (1, 7)]
+    for k, i in turns:
+        for d in (2, 1, 3):
+            to = (y + d) % NY
+            tx[k, i, to] = acc[k, groups[i], to].astype(BF16)
+            send(tx.at[k, i, to], rx.at[k, i, y], rsend, rrecv.at[k, i], device(x, to, z, c))
+    spread_word(3)
+
+    for k, i in turns:
+        g = groups[i]
+        with scope("r%d%d_y" % (k, i)):
+            wait_for(rx.at[k, i, pl.ds(0, 3)], rrecv.at[k, i])
+        total = acc[k, g, y]
+        for d in (1, 2, 3):
+            total += rx[k, i, (y + d) % NY].astype(F32)
+        zs[k, i] = total.astype(BF16).reshape(2, 16, 128)
+        for b in (0, 1) if i < pairs - 1 else (1 - zb,):
+            send(zs.at[k, i, b], zr.at[k, z], zsend, zrecv.at[k], device(x, y, g * 2 + b, c))
     for k in range(2):
-        for i, g in enumerate(groups):
-            for d in (2, 1, 3):
-                to = (y + d) % NY
-                tx[k, i, to] = acc[k, g, to].astype(BF16)
-                send(tx.at[k, i, to], rx.at[k, i, y], rsend, rrecv.at[k, i], device(x, to, z, c))
-    spread_word(3)
-
-    def along_z(k):
-        for i, g in enumerate(groups):
-            with scope("r%d%d_y" % (k, i)):
-                wait_for(rx.at[k, i, pl.ds(0, 3)], rrecv.at[k, i])
-            total = acc[k, g, y]
-            for d in (1, 2, 3):
-                total += rx[k, i, (y + d) % NY].astype(F32)
-            zs[k, i] = total.astype(BF16).reshape(2, 16, 128)
-            for b in (0, 1) if i < pairs - 1 else (1 - zb,):
-                send(zs.at[k, i, b], zr.at[k, z], zsend, zrecv.at[k], device(x, y, g * 2 + b, c))
         zr[k, z] = zs[k, pairs - 1, zb]
 
     def back_along_z(k):
@@ -313,8 +311,6 @@
                     at = h * half + n * wide + i * 128
                     out[k : k + 1, at : at + 128] = whole[i : i + 1]
 
-    along_z(0)
-    along_z(1)
     back_along_z(0)
     back_along_z(1)
     back_along_y(0)
@@ -346,6 +342,7 @@
     sources, detectors = rows * lax.axis_size("blk"), det_fields.shape[0] * lax.axis_size("blk")
     scale = 1.0 / (sources * detectors)
     hbm = pl.BlockSpec(memory_space=pl.ANY)
+    given = [pltpu.with_memory_space_constraint(a, pltpu.HBM) for a in (src_fields, det_fields, probes)]
     return pl.pallas_call(
         functools.partial(kernel, scale),
         out_shape=jax.ShapeDtypeStruct((2, voxels), F32),
@@ -370,14 +367,14 @@
             pltpu.VMEM((2, 2, NX * NC, NB, half // NB // 128, 128), F32),
             DMA((NQ + 1,)),
             DMA((3,)),
-            DMA((NQ + 1,)),
-            DMA((NQ + 1,)),
+            DMA((NQ + 2,)),
+            DMA((NQ + 2,)),
             DMA,
             DMA((4,)),
-            DMA((NQ + 1,)),
-            DMA((NQ + 1,)),
-            DMA((NQ + 1,)),
-            DMA((NQ + 1,)),
+            DMA((NQ + 2,)),
+            DMA((NQ + 2,)),
+            DMA((NQ + 2,)),
+            DMA((NQ + 2,)),
             DMA,
             DMA((2, 8)),
             DMA,
@@ -391,10 +388,10 @@
             pltpu.SemaphoreType.REGULAR((3,)),
         ],
         compiler_params=pltpu.CompilerParams(
-            collective_id=0, has_side_effects=True, vmem_limit_bytes=60 * 2**20
+            collective_id=0, has_side_effects=True, vmem_limit_bytes=50_000_000
         ),
         name="gauss_newton",
-    )(src_fields, det_fields, probes)
+    )(*given)
 
 
 def solution(mesh):

time: 65.5 us -> 65.5 us (level)
  Pallas kernels: 63.9 us -> 64.7 us
  local copies, waits for them, and re-layouts: 1.38 us -> 0.62 us
    pallas_call x1, Pallas kernels: 63.9 us -> 64.7 us  [shards(): pl.pallas_call(functools.partial(kernel, scale), out_shape=jax.ShapeDtype...]
    unnamed x1, local copies, waits for them, and re-layouts: 1.38 us -> 0.62 us
where the time goes in v5:
time: 65.5 us; the launch traced here: 65.3 us
  Pallas kernels  64.7 us (99%)
    pallas_call x1, Pallas kernels, shards(): pl.pallas_call(functools.partial(kernel, scale), out_shape=jax.ShapeDtype...  64.7 us

profile of v5, /device:TPU:1, one launch (start us, length us, event | category | flops | bytes accessed | tf_op | source)
XLA Modules:
  0.0 65.3 jit_solution(3954306115468059911)
XLA Ops:
  0.0 64.7 %gauss_newton.1 = f32[2,4096]{1,0:T(2,128)S(1)} custom-call(bf16[64,4096]{1,0:T(8,128)(2,1)} %src_hbm.1, bf16[64,4096]{1,0:T(8,128)(2,1)} %det_hbm.1, bf16[2,4096]{1,0:T(2,128)(2,1)} %probes_hbm.1), custom_call_target="tpu_custom_call" | custom-call | tf_op jit(solution)/shard_map/gauss_newton/pallas_call | solution.py:346
  64.7 0.6 copy.5

commit v6 on v5

--- a/solution.py
+++ b/solution.py
@@ -43,6 +43,8 @@
     pr_in,
     S,
     D,
+    XS,
+    XD,
     acc,
     tx,
     rx,
@@ -54,15 +56,18 @@
     cv,
     ob,
     ld,
+    pl_sem,
     ysend,
     yS,
     yD,
     pS,
     xsend,
-    xS,
     xD,
-    c0,
-    c1,
+    whole,
+    bsend,
+    brecv,
+    yB,
+    cB,
     rsend,
     rrecv,
     zsend,
@@ -105,21 +110,23 @@
 
     h_up, h_down = up // 2, down // 2
 
-    parts = []
+    parts, turned = [], []
     for q in range(NQ):
-        cuts = 2 if q in (0, NQ - 1) else 1
-        parts += [(q, i * vc // cuts, vc // cuts) for i in range(cuts)]
+        cuts = 2 if q in (0, NQ - 2) else 1
+        for i in range(cuts):
+            late = q == NQ - 1 or (q == NQ - 2 and i == 1)
+            (turned if late else parts).append((q, i * vc // cuts, vc // cuts))
     last = len(parts)
 
     def columns(h, q, lo, wide):
         return pl.ds(pl.multiple_of(h * half + q * vc + lo, wide), wide)
 
-    pltpu.make_async_copy(probes_hbm, pr_v, ld.at[NQ]).start()
-    for q in range(0, NQ, 2):
+    pltpu.make_async_copy(probes_hbm, pr_v, pl_sem).start()
+    for q in (0, NQ - 2, *range(2, NQ - 2, 2)):
         for h in range(2):
             at = pl.ds(h * half + q * vc, 2 * vc)
-            pltpu.make_async_copy(det_hbm.at[:, at], det_v.at[:, at], ld.at[q]).start()
-            pltpu.make_async_copy(src_hbm.at[:, at], src_v.at[:, at], ld.at[q + 1]).start()
+            pltpu.make_async_copy(det_hbm.at[:, at], det_v.at[:, at], ld.at[q // 2, 0]).start()
+            pltpu.make_async_copy(src_hbm.at[:, at], src_v.at[:, at], ld.at[q // 2, 1]).start()
     with scope("t_barrier"):
         pl.semaphore_wait(barrier, len(near))
 
@@ -135,8 +142,8 @@
     own, other = pl.ds(0, 128), pl.ds(128, 128)
     def swap(fields, here, i, sem, n):
         q, lo, wide = parts[n]
-        if q % 2 == 0 and lo == 0:
-            wait_for(D.at[q, pl.ds(0, 256)], ld.at[q + i])
+        if q % 2 == 0 and lo == 0 and q < NQ - 2:
+            wait_for(D.at[q, pl.ds(0, 256)], ld.at[q // 2, i])
         to = (q, mine, pl.ds(lo, wide))
         send(fields.at[:, columns(h_up, q, lo, wide)], here.at[to], ysend.at[i], sem.at[n], dev_up)
         send(fields.at[:, columns(h_down, q, lo, wide)], here.at[to], ysend.at[i], sem.at[n], dev_down)
@@ -145,7 +152,7 @@
         swap(det_v, D, 0, yD, t)
         swap(src_v, S, 1, yS, t)
         if t == 0:
-            wait_for(pr_v, ld.at[NQ])
+            wait_for(pr_v, pl_sem)
             send(
                 pr_v.at[:, pl.ds(pl.multiple_of(h_up * half, half), half)],
                 pr_in,
@@ -154,29 +161,54 @@
                 dev_up,
             )
             spread_word(0)
+        if t == 2:
+            for i, (fields, there, to) in enumerate(((det_v, XD, dev_xd), (src_v, XS, dev_xs))):
+                wait_for(D.at[0, pl.ds(0, 256)], ld.at[NQ // 2 - 1, i])
+                for h in range(2):
+                    at = pl.ds(h * half + turned[0][0] * vc + turned[0][1], there.shape[2])
+                    send(fields.at[:, at], there.at[h], bsend.at[i], brecv.at[i], to)
+
+    theirs = pl.ds(pl.multiple_of(128 + yh * 64, 64), 64)
+
+    def swap_b():
+        start = 0
+        for n, (q, lo, wide) in enumerate(turned):
+            for i, (fields, x_in, here) in enumerate(((det_v, XD, D), (src_v, XS, S))):
+                at, x_at = pl.ds(lo, wide), pl.ds(start, wide)
+                for h, to in ((h_up, dev_up), (h_down, dev_down)):
+                    send(fields.at[:, columns(h, q, lo, wide)], here.at[q, mine, at], ysend.at[i], yB.at[i, n], to)
+                if n == 0:
+                    wait_for(x_in, brecv.at[i])
+                for h, to in ((h_up, dev_up), (h_down, dev_down)):
+                    send(x_in.at[h, :, x_at], here.at[q, theirs, at], bsend.at[2 + i], yB.at[i, n], to)
+            start += wide
+
+    def pass_b(n):
+        q, at = turned[n][0], pl.ds(*turned[n][1:])
+        wait_for(D.at[q, pl.ds(0, 256), at], yB.at[0, n])
+        send(D.at[q, pl.ds(0, 256), at], D.at[q, pl.ds(256, 256), at], xsend.at[2], cB.at[n], dev_c)
 
     def pass_own(n):
         q, at = parts[n][0], pl.ds(*parts[n][1:])
         wait_for(D.at[q, own, at], yD.at[n])
         send(D.at[q, own, at], D.at[q, other, at], xsend.at[1], xD.at[n], dev_xd)
-        send(D.at[q, own, at], D.at[q, pl.ds(256, 128), at], xsend.at[2], c0.at[n], dev_c)
-        if n == last - 1:
-            send(D.at[q, own, at], D.at[q, pl.ds(384, 128), at], xsend.at[3], c1.at[n], device(xd, y, z, 1 - c))
+        send(D.at[q, own, at], D.at[q, pl.ds(256, 128), at], xsend.at[3], whole.at[n], dev_c)
         wait_for(S.at[q, own, at], yS.at[n])
-        send(S.at[q, own, at], S.at[q, other, at], xsend.at[0], xS.at[n], dev_xs)
+        send(S.at[q, own, at], S.at[q, other, at], xsend.at[0], whole.at[n], dev_xs)
 
     def pass_other(n):
         q, at = parts[n][0], pl.ds(*parts[n][1:])
         wait_for(D.at[q, other, at], xD.at[n])
-        if n < last - 1:
-            send(D.at[q, other, at], D.at[q, pl.ds(384, 128), at], xsend.at[3], c1.at[n], dev_c)
+        send(D.at[q, other, at], D.at[q, pl.ds(384, 128), at], xsend.at[4], whole.at[n], dev_c)
 
     def measure(n):
-        q, lo, wide = parts[n]
+        q, lo, wide = (parts + turned)[n]
         at = pl.ds(lo, wide)
-        wait_for(D.at[q, pl.ds(256, 128), at], c0.at[n])
-        wait_for(D.at[q, pl.ds(384, 128), at], c1.at[n])
-        wait_for(S.at[q, other, at], xS.at[n])
+        if n < last:
+            wait_for(D.at[q, pl.ds(0, 384), at], whole.at[n])
+        else:
+            wait_for(D.at[q, pl.ds(256, 256), at], cB.at[n - last])
+            wait_for(S.at[q, :, at], yB.at[1, n - last])
         fields = S[q, :, at].astype(F32)
         p = pr_in[:, q * vc + lo : q * vc + lo + wide].astype(F32)
         det = D[q, :, at]
@@ -192,19 +224,25 @@
                         acc[k, 2 * g + h] = piece[:, h]
 
     word = {3: 1, 6: 2}
-    for t in range(last + 6):
+    for t in range(last + 8):
         if t < last:
             with scope("g%02d_own" % t):
                 pass_own(t)
+        if t == 3:
+            with scope("g%02d_b" % t):
+                swap_b()
         if t in word:
             with scope("g%02d_word" % t):
                 spread_word(word[t])
+        if t - last in (0, 1):
+            with scope("g%02d_b" % t):
+                pass_b(t - last)
         if 0 <= t - 4 < last:
             with scope("g%02d_other" % t):
                 pass_other(t - 4)
         if t == 6:
             wait_for(pr_in, pS)
-        if 0 <= t - 6 < last:
+        if 0 <= t - 6 < last + 2:
             with scope("g%02d_meas" % t):
                 measure(t - 6)
 
@@ -213,8 +251,7 @@
     s = 1 - 2 * zb
     away = (4, 3 * s, -3 * s, 2 * s, -2 * s, s, -s, 0)
     groups = [(zp + pairs + o) % pairs for o in away]
-    turns = [(0, 0), (0, 1), (0, 2), (1, 0), (1, 1), (1, 2), (0, 3), (0, 4), (1, 3), (1, 4)]
-    turns += [(0, 5), (0, 6), (0, 7), (1, 5), (1, 6), (1, 7)]
+    turns = [(k, i) for k in range(2) for i in range(pairs)]
     for k, i in turns:
         for d in (2, 1, 3):
             to = (y + d) % NY
@@ -247,21 +284,22 @@
             for to in (step, -step)[: 1 if step == NZ // 2 else 2]:
                 send(mz.at[k], M.at[k, zp, y, zb], gsend, grecv.at[k, zp], dev_z(to))
 
+    block, side = zp // 2, 2 * (zp % 2) - 1
+    blocks = [(block + o) % 4 for o in (0, 4 + side, 4 - side, 2)]
+
     back = groups[::-1]
 
     def back_along_y(k):
         for i, g in enumerate(back):
             with scope("b%d%d_z" % (k, i)):
                 wait_for(zr.at[k, pl.ds(0, 2 if i else 1)], grecv.at[k, g])
+            off = (g // 2 - block + 4) % 4
+            far = jnp.where((off == 0) | (off == (4 + side) % 4), 0, 1)
             for d in (2, 1, 3):
-                send(M.at[k, g, y], M.at[k, g, y], asend, arecv.at[k, g], device(x, (y + d) % NY, z, c))
-
-    block, side = zp // 2, 2 * (zp % 2) - 1
-    blocks = [(block + o) % 4 for o in (0, 4 + side, 4 - side, 2)]
-
-    def arrived(k, g):
-        for h in range(2):
-            wait_for(M.at[k, 2 * g + h, pl.ds(0, 3)], arecv.at[k, 2 * g + h])
+                send(M.at[k, g, y], M.at[k, g, y], asend, arecv.at[k, far], device(x, (y + d) % NY, z, c))
+
+    def arrived(k, far):
+        wait_for(M.at[k, pl.ds(0, 4), pl.ds(0, 3)], arecv.at[k, far])
 
     def contribution(k, q, lo):
         two = blocks[lo : lo + 2]
@@ -276,15 +314,13 @@
 
     def front(k):
         with scope("m%d_front" % k):
-            arrived(k, blocks[0])
-            arrived(k, blocks[1])
+            arrived(k, 0)
             for q in range(NQ):
                 part[k, q] = contribution(k, q, 0)
 
     def rest(k):
         with scope("m%d_y" % k):
-            arrived(k, blocks[2])
-            arrived(k, blocks[3])
+            arrived(k, 1)
         per = NQ // NB
         with scope("m%d_rest" % k):
             for n in range(NB):
@@ -303,13 +339,13 @@
         wide = half // NB
         for h in range(2):
             for n in range(NB):
-                whole = ob[k, h, 0, n]
+                total = ob[k, h, 0, n]
                 for e in range(1, NX * NC):
-                    whole += ob[k, h, e, n]
-                whole = whole * scale
+                    total += ob[k, h, e, n]
+                total = total * scale
                 for i in range(wide // 128):
                     at = h * half + n * wide + i * 128
-                    out[k : k + 1, at : at + 128] = whole[i : i + 1]
+                    out[k : k + 1, at : at + 128] = total[i : i + 1]
 
     back_along_z(0)
     back_along_z(1)
@@ -325,9 +361,12 @@
     wait_for(det_v, ysend.at[0])
     wait_for(src_v, ysend.at[1])
     wait_for(pr_in, ysend.at[2])
-    wait_for(S.at[:, own], xsend.at[0])
-    for i in (1, 2, 3):
-        wait_for(D.at[:, own], xsend.at[i])
+    passed = det_v.at[:, pl.ds(0, 2 * sum(wide for _, _, wide in parts))]
+    for i in (0, 1, 3, 4):
+        wait_for(passed, xsend.at[i])
+    wait_for(det_v.at[:, pl.ds(0, 4 * sum(wide for _, _, wide in turned))], xsend.at[2])
+    for i in range(4):
+        wait_for(XD, bsend.at[i])
     wait_for(tx.at[:, :, pl.ds(0, 3)], rsend)
     wait_for(zr.at[:, pl.ds(0, NZ - 1)], zsend)
     wait_for(zr.at[:, pl.ds(0, NZ - 1)], gsend)
@@ -355,6 +394,8 @@
             pltpu.VMEM((2, half), BF16),
             pltpu.VMEM((NQ, 256, vc), BF16),
             pltpu.VMEM((NQ, 512, vc), BF16),
+            pltpu.VMEM((2, 64, 3 * vc // 2), BF16),
+            pltpu.VMEM((2, 64, 3 * vc // 2), BF16),
             pltpu.VMEM((2, 8, 4, 32, 128), F32),
             pltpu.VMEM((2, 8, 4, 32, 128), BF16),
             pltpu.VMEM((2, 8, 4, 32, 128), BF16),
@@ -365,16 +406,19 @@
             pltpu.VMEM((2, NQ, 8, vc), F32),
             pltpu.VMEM((2, NB, half // NB // 128, 128), F32),
             pltpu.VMEM((2, 2, NX * NC, NB, half // NB // 128, 128), F32),
-            DMA((NQ + 1,)),
+            DMA((NQ // 2, 2)),
+            DMA,
             DMA((3,)),
-            DMA((NQ + 2,)),
-            DMA((NQ + 2,)),
-            DMA,
+            DMA((NQ,)),
+            DMA((NQ,)),
+            DMA,
+            DMA((5,)),
+            DMA((NQ,)),
+            DMA((NQ,)),
             DMA((4,)),
-            DMA((NQ + 2,)),
-            DMA((NQ + 2,)),
-            DMA((NQ + 2,)),
-            DMA((NQ + 2,)),
+            DMA((2,)),
+            DMA((2, 2)),
+            DMA((2,)),
             DMA,
             DMA((2, 8)),
             DMA,
@@ -382,7 +426,7 @@
             DMA,
             DMA((2, 8)),
             DMA,
-            DMA((2, 8)),
+            DMA((2, 2)),
             DMA,
             DMA((2,)),
             pltpu.SemaphoreType.REGULAR((3,)),

time: 65.5 us -> 62.6 us (0.956)
  Pallas kernels: 64.7 us -> 61.8 us
    pallas_call x1, Pallas kernels: 64.7 us -> 61.8 us  [shards(): pl.pallas_call(functools.partial(kernel, scale), out_shape=jax.ShapeDtype...]
where the time goes in v6:
time: 62.6 us; the launch traced here: 62.4 us
  Pallas kernels  61.8 us (99%)
    pallas_call x1, Pallas kernels, shards(): pl.pallas_call(functools.partial(kernel, scale), out_shape=jax.ShapeDtype...  61.8 us

profile of v6, /device:TPU:1, one launch (start us, length us, event | category | flops | bytes accessed | tf_op | source)
XLA Modules:
  0.0 62.4 jit_solution(11932094105645141162)
XLA Ops:
  0.0 61.8 %gauss_newton.1 = f32[2,4096]{1,0:T(2,128)S(1)} custom-call(bf16[64,4096]{1,0:T(8,128)(2,1)} %src_hbm.1, bf16[64,4096]{1,0:T(8,128)(2,1)} %det_hbm.1, bf16[2,4096]{1,0:T(2,128)(2,1)} %probes_hbm.1), custom_call_target="tpu_custom_call" | custom-call | tf_op jit(solution)/shard_map/gauss_newton/pallas_call | solution.py:385
  61.8 0.6 copy.5

commit v7 on v6

--- a/solution.py
+++ b/solution.py
@@ -223,28 +223,28 @@
                     else:
                         acc[k, 2 * g + h] = piece[:, h]
 
-    word = {3: 1, 6: 2}
-    for t in range(last + 8):
-        if t < last:
-            with scope("g%02d_own" % t):
-                pass_own(t)
+    steps = []
+    for t in range(last):
+        steps.append((pass_own, t))
         if t == 3:
-            with scope("g%02d_b" % t):
-                swap_b()
-        if t in word:
-            with scope("g%02d_word" % t):
-                spread_word(word[t])
-        if t - last in (0, 1):
-            with scope("g%02d_b" % t):
-                pass_b(t - last)
-        if 0 <= t - 4 < last:
-            with scope("g%02d_other" % t):
-                pass_other(t - 4)
+            steps.append((spread_word, 1))
         if t == 6:
+            steps.append((spread_word, 2))
+        if t >= 3:
+            steps.append((pass_other, t - 3))
+        if t >= 5:
+            steps.append((measure, t - 5))
+    n = last
+    steps += [(pass_other, n - 3), (pass_b, 0), (measure, n - 5), (measure, n - 4), (pass_other, n - 2)]
+    steps += [(measure, n - 3), (measure, n), (pass_other, n - 1), (pass_b, 1)]
+    steps += [(measure, n - 2), (measure, n - 1), (measure, n + 1)]
+    for t, (step, n) in enumerate(steps):
+        if step is measure and n == 0:
             wait_for(pr_in, pS)
-        if 0 <= t - 6 < last + 2:
-            with scope("g%02d_meas" % t):
-                measure(t - 6)
+        with scope("g%02d_%s%d" % (t, step.__name__, n)):
+            step(n)
+        if step is pass_own and n == 3:
+            swap_b()
 
     pairs = NZ // 2
     zp, zb = z // 2, z % 2

time: 62.6 us -> 61.6 us (0.984)
  Pallas kernels: 61.8 us -> 60.8 us
    pallas_call x1, Pallas kernels: 61.8 us -> 60.8 us  [shards(): pl.pallas_call(functools.partial(kernel, scale), out_shape=jax.ShapeDtype...]
where the time goes in v7:
time: 61.6 us; the launch traced here: 61.5 us
  Pallas kernels  60.8 us (99%)
  local copies, waits for them, and re-layouts  0.62 us (1%)
    pallas_call x1, Pallas kernels, shards(): pl.pallas_call(functools.partial(kernel, scale), out_shape=jax.ShapeDtype...  60.8 us

profile of v7, /device:TPU:1, one launch (start us, length us, event | category | flops | bytes accessed | tf_op | source)
XLA Modules:
  0.0 61.5 jit_solution(9955127049283238742)
XLA Ops:
  0.0 60.8 %gauss_newton.1 = f32[2,4096]{1,0:T(2,128)S(1)} custom-call(bf16[64,4096]{1,0:T(8,128)(2,1)} %src_hbm.1, bf16[64,4096]{1,0:T(8,128)(2,1)} %det_hbm.1, bf16[2,4096]{1,0:T(2,128)(2,1)} %probes_hbm.1), custom_call_target="tpu_custom_call" | custom-call | tf_op jit(solution)/shard_map/gauss_newton/pallas_call | solution.py:385
  60.8 0.6 %copy.5 = f32[2,4096]{1,0:T(2,128)} copy(f32[2,4096]{1,0:T(2,128)S(1)} %gauss_newton.1) | data formatting | bytes 65536

commit v8 on v7

--- a/solution.py
+++ b/solution.py
@@ -90,8 +90,8 @@
     scope = jax.named_scope
 
     up, down = (y + 1) % NY, (y + 3) % NY
-    xs = (x // 2) * 2 + 1 - x % 2
-    xd = 3 - x
+    xd = (x // 2) * 2 + 1 - x % 2
+    xs = 3 - x
     me = x * 2 + c
     dev_up, dev_down = device(x, up, z, c), device(x, down, z, c)
     dev_xs, dev_xd = device(xs, y, z, c), device(xd, y, z, c)
@@ -356,7 +356,6 @@
     front(1)
     rest(1)
     finish(0)
-    finish(1)
 
     wait_for(det_v, ysend.at[0])
     wait_for(src_v, ysend.at[1])
@@ -372,6 +371,7 @@
     wait_for(zr.at[:, pl.ds(0, NZ - 1)], gsend)
     wait_for(M.at[:, :, pl.ds(0, 3)], asend)
     wait_for(ob, fsend)
+    finish(1)
 
 
 def shards(src_fields, det_fields, probes):

time: 61.6 us -> 62 us (level)
  no operation moved by 1% of the time
where the time goes in v8:
time: 62 us; the launch traced here: 61.9 us
  Pallas kernels  61.3 us (99%)
  local copies, waits for them, and re-layouts  0.62 us (1%)
    pallas_call x1, Pallas kernels, shards(): pl.pallas_call(functools.partial(kernel, scale), out_shape=jax.ShapeDtype...  61.3 us

profile of v8, /device:TPU:1, one launch (start us, length us, event | category | flops | bytes accessed | tf_op | source)
XLA Modules:
  0.0 61.9 jit_solution(7511038552223599304)
XLA Ops:
  0.0 61.3 %gauss_newton.1 = f32[2,4096]{1,0:T(2,128)S(1)} custom-call(bf16[64,4096]{1,0:T(8,128)(2,1)} %src_hbm.1, bf16[64,4096]{1,0:T(8,128)(2,1)} %det_hbm.1, bf16[2,4096]{1,0:T(2,128)(2,1)} %probes_hbm.1), custom_call_target="tpu_custom_call" | custom-call | tf_op jit(solution)/shard_map/gauss_newton/pallas_call | solution.py:385
  61.3 0.6 copy.5

commit v9 on v8

--- a/solution.py
+++ b/solution.py
@@ -329,9 +329,11 @@
                     row = jnp.sum(part[k, q] + contribution(k, q, 2), axis=0, keepdims=True)
                     rows += [row[:, i * 128 : (i + 1) * 128] for i in range(vc // 128)]
                 cv[k, n] = jnp.concatenate(rows, axis=0)
-                for e in range(NX * NC):
-                    for to in (up, down):
-                        send(cv.at[k, n], ob.at[k, yh, me, n], fsend, frecv.at[k], device(e // 2, to, z, e % 2))
+                for d in (2, 1, 3, 0):
+                    for core in range(NC):
+                        for to in (up, down):
+                            at = device((x + d) % NX, to, z, core)
+                            send(cv.at[k, n], ob.at[k, yh, me, n], fsend, frecv.at[k], at)
 
     def finish(k):
         with scope("f%d_recv" % k):

time: 62 us -> 62 us (level)
  no operation moved by 1% of the time
where the time goes in v9:
time: 62 us; the launch traced here: 61.9 us
  Pallas kernels  61.2 us (99%)
  local copies, waits for them, and re-layouts  0.62 us (1%)
    pallas_call x1, Pallas kernels, shards(): pl.pallas_call(functools.partial(kernel, scale), out_shape=jax.ShapeDtype...  61.2 us

profile of v9, /device:TPU:1, one launch (start us, length us, event | category | flops | bytes accessed | tf_op | source)
XLA Modules:
  0.0 61.9 jit_solution(7619829624197098611)
XLA Ops:
  0.0 61.2 %gauss_newton.1 = f32[2,4096]{1,0:T(2,128)S(1)} custom-call(bf16[64,4096]{1,0:T(8,128)(2,1)} %src_hbm.1, bf16[64,4096]{1,0:T(8,128)(2,1)} %det_hbm.1, bf16[2,4096]{1,0:T(2,128)(2,1)} %probes_hbm.1), custom_call_target="tpu_custom_call" | custom-call | tf_op jit(solution)/shard_map/gauss_newton/pallas_call | solution.py:387
  61.2 0.6 copy.5

commit v10 on v9

--- a/solution.py
+++ b/solution.py
@@ -280,7 +280,7 @@
             total += zr[k, j].astype(F32)
         mz[k] = total.astype(BF16)
         M[k, zp, y, zb] = mz[k]
-        for step in range(NZ // 2, 0, -1):
+        for step in range(NZ // 2, 0, -1) if k else range(1, NZ // 2 + 1):
             for to in (step, -step)[: 1 if step == NZ // 2 else 2]:
                 send(mz.at[k], M.at[k, zp, y, zb], gsend, grecv.at[k, zp], dev_z(to))
 

time: 62 us -> 62.1 us (level)
  no operation moved by 1% of the time
where the time goes in v10:
time: 62.1 us; the launch traced here: 62 us
  Pallas kernels  61.3 us (99%)
    pallas_call x1, Pallas kernels, shards(): pl.pallas_call(functools.partial(kernel, scale), out_shape=jax.ShapeDtype...  61.3 us

profile of v10, /device:TPU:1, one launch (start us, length us, event | category | flops | bytes accessed | tf_op | source)
XLA Modules:
  0.0 62.0 jit_solution(3868437497789884408)
XLA Ops:
  0.0 61.3 %gauss_newton.1 = f32[2,4096]{1,0:T(2,128)S(1)} custom-call(bf16[64,4096]{1,0:T(8,128)(2,1)} %src_hbm.1, bf16[64,4096]{1,0:T(8,128)(2,1)} %det_hbm.1, bf16[2,4096]{1,0:T(2,128)(2,1)} %probes_hbm.1), custom_call_target="tpu_custom_call" | custom-call | tf_op jit(solution)/shard_map/gauss_newton/pallas_call | solution.py:387
  61.3 0.6 copy.5
